TPU v7x, 256 devices: a whole 4x4x8 slice. The times are simulated.
256 devices in a mesh: gx: 8 (over x, core), gy: 8 (over z), gz: 4 (over y).
Axes of the slice: x: 4, y: 4, z: 8, core: 2. Of those that a mesh axis runs over, the one named last changes fastest.
Arguments:
- particle_mass: float32 [8388608], P(('gx', 'gy', 'gz')), may hold values from 0.5 to 2
- particle_velocity: float32 [3, 8388608], P(None, ('gx', 'gy', 'gz')), may hold values from -6 to 6
- particle_affine: float32 [9, 8388608], P(None, ('gx', 'gy', 'gz')), may hold values from -6 to 6
- particle_cell: int32 [3, 8388608], P(None, ('gx', 'gy', 'gz')), may hold values from 0 to 13
- particle_fraction: int32 [3, 8388608], P(None, ('gx', 'gy', 'gz')), may hold values from 0 to 1023
- block_owner: int32 [16384, 1], P(('gx', 'gy', 'gz')), may hold values from 0 to 31; in each aligned block of 64 rows (0 to 63, 64 to 127, ...) at most 4 rows name the same one
- block_slot: int32 [16384], P(('gx', 'gy', 'gz')), may hold values from 0 to 15
- block_count: int32 [16384], P(('gx', 'gy', 'gz')), may hold values from 128 to 512
- cell_drag: float32 [4096, 4096], P(('gx', 'gy', 'gz')), may hold values from 0.5 to 2
Outputs:
- grid_velocity: float32 [4096, 3, 4096], P(('gx', 'gy', 'gz'))
- new_velocity: float32 [3, 8388608], P(None, ('gx', 'gy', 'gz'))
- new_affine: float32 [9, 8388608], P(None, ('gx', 'gy', 'gz'))
Inputs may be any that keep to these rules, and one draw needn't show every extreme that they name: `block_owner`: owner index counted over the devices with the particle device's own gx index, in gy+gz order; among the rows of one device, no owner is named more than 4 times. `block_count`: slots at or beyond the count are absent. `particle_cell`: A particle's three stencil nodes lie inside its grid block.
All inputs are finite; a program needn't handle non-finite values.
Results may differ from a plain program's by a relative error of at most 0.0085.
Values may be sent and summed in bfloat16 or wider, within the bound.
No kernel may reach another device: no remote copies, remote signals or barrier semaphores. Data moves between devices by JAX's collectives and lax.ppermute only.
A program may use at most 128 MiB of HBM per device.

v0:
```python
import jax
import jax.numpy as jnp
from jax import lax
from jax.sharding import PartitionSpec as P

EDGE = 16
QUANT = 1024


batch_blocks = 4


def spline(offset):
    magnitude = jnp.abs(offset)
    inner_part = 0.75 - magnitude * magnitude
    outer_part = 0.5 * (1.5 - magnitude) * (1.5 - magnitude)
    return jnp.where(magnitude < 0.5, inner_part, jnp.where(magnitude < 1.5, outer_part, 0.0))


def particle_table(
    particle_mass, particle_velocity, particle_affine, particle_cell, particle_fraction, block_count
):
    blocks = block_count.shape[0]
    batch_shape = (blocks, particle_mass.shape[0] // blocks)
    places = jnp.arange(batch_shape[1], dtype=jnp.int32)
    present = places[None, :] < block_count[:, None]
    live_mass = jnp.where(present, particle_mass.reshape(batch_shape), 0.0)
    position = (
        particle_cell.astype(jnp.float32)
        + 0.5
        + (particle_fraction.astype(jnp.float32) + 0.5) / QUANT
    )
    return jnp.concatenate(
        [
            live_mass[None],
            particle_velocity.reshape((3,) + batch_shape),
            particle_affine.reshape((9,) + batch_shape),
            position.reshape((3,) + batch_shape),
        ],
        axis=0,
    )


def stencil(particle_data):
    node_coords = jnp.arange(EDGE, dtype=jnp.float32)
    offset = node_coords[None, :, None, None] - particle_data[13:16][:, None]
    weights = spline(offset)
    return (weights, weights * offset)


def planes(weights, slopes):

    def outer(first_factor, second_factor):
        product_table = first_factor[:, None] * second_factor[None, :]
        return product_table.reshape((EDGE * EDGE,) + product_table.shape[2:]).astype(jnp.bfloat16)

    return (
        outer(weights[1], weights[2]),
        outer(slopes[1], weights[2]),
        outer(weights[1], slopes[2]),
    )


def deposit(particle_data):
    batch_shape = particle_data.shape[1:]
    weights, slopes = stencil(particle_data)
    plane_zero, plane_one, plane_two = planes(weights, slopes)
    live_mass = particle_data[0]
    along_x = weights[0]
    slope_x = slopes[0]
    affine = particle_data[4:13].reshape((3, 3) + batch_shape)
    mass_lead = (live_mass[None] * along_x)[None]
    momentum_lead = live_mass[None, None] * (
        particle_data[1:4][:, None] * along_x[None] + affine[:, 0][:, None] * slope_x[None]
    )
    lead_zero = jnp.concatenate([mass_lead, momentum_lead], axis=0).astype(jnp.bfloat16)
    lead_one = (live_mass[None, None] * affine[:, 1][:, None] * along_x[None]).astype(jnp.bfloat16)
    lead_two = (live_mass[None, None] * affine[:, 2][:, None] * along_x[None]).astype(jnp.bfloat16)

    def contract(lead, plane):
        flattened = lead.reshape((-1,) + batch_shape)
        return jnp.einsum("anp,bnp->nab", flattened, plane, preferred_element_type=jnp.float32)

    count_blocks = batch_shape[0]
    dep_zero = contract(lead_zero, plane_zero).reshape(count_blocks, 4, -1)
    dep_one = contract(lead_one, plane_one).reshape(count_blocks, 3, -1)
    dep_two = contract(lead_two, plane_two).reshape(count_blocks, 3, -1)
    return jnp.concatenate([dep_zero[:, :1], dep_zero[:, 1:] + dep_one + dep_two], axis=1)


def interpolate(particle_data, grid_rows):
    batch_shape = particle_data.shape[1:]
    weights, slopes = stencil(particle_data)
    plane_zero, plane_one, plane_two = planes(weights, slopes)
    along_x = weights[0]
    slope_x = slopes[0]
    flattened = grid_rows.reshape(batch_shape[0], 3 * EDGE, EDGE * EDGE)

    def contract(plane):
        moment = jnp.einsum("nab,bnp->anp", flattened, plane, preferred_element_type=jnp.float32)
        return moment.reshape((3, EDGE) + batch_shape)

    moment_zero = contract(plane_zero)
    moment_one = contract(plane_one)
    moment_two = contract(plane_two)
    velocity_out = jnp.sum(along_x[None] * moment_zero, axis=1)
    column_zero = 4.0 * jnp.sum(slope_x[None] * moment_zero, axis=1)
    column_one = 4.0 * jnp.sum(along_x[None] * moment_one, axis=1)
    column_two = 4.0 * jnp.sum(along_x[None] * moment_two, axis=1)
    affine_out = jnp.stack([column_zero, column_one, column_two], axis=1).reshape(
        (9,) + batch_shape
    )
    present = (particle_data[0] > 0.0).astype(jnp.float32)
    return jnp.concatenate([velocity_out, affine_out], axis=0) * present[None]


def deposit_all(particle_data):
    block_total = particle_data.shape[1]

    def deposit_advance(state_carry, step_index):
        portion = lax.dynamic_slice_in_dim(
            particle_data, step_index * batch_blocks, batch_blocks, 1
        )
        return (state_carry, deposit(portion))

    unused, stacked = lax.scan(
        deposit_advance,
        jnp.zeros((), jnp.float32),
        jnp.arange(block_total // batch_blocks, dtype=jnp.int32),
    )
    return stacked.reshape((block_total,) + stacked.shape[2:])


def interpolate_all(particle_data, grid_rows):
    block_total = particle_data.shape[1]

    def interpolate_advance(step_index, result):
        first_block = step_index * batch_blocks
        portion = lax.dynamic_slice_in_dim(particle_data, first_block, batch_blocks, 1)
        cell_rows = lax.dynamic_slice_in_dim(grid_rows, first_block, batch_blocks, 0)
        return lax.dynamic_update_slice_in_dim(
            result, interpolate(portion, cell_rows), first_block, 1
        )

    initial = jnp.zeros((12, block_total, particle_data.shape[2]), jnp.float32)
    return lax.fori_loop(0, block_total // batch_blocks, interpolate_advance, initial)


def send_slots(owners, group_size, capacity):
    targets = jnp.arange(group_size, dtype=jnp.int32)
    matches = (owners[:, None] == targets[None, :]).astype(jnp.int32)
    earlier = jnp.cumsum(matches, axis=0) - matches
    ranking = jnp.sum(earlier * matches, axis=1)
    return owners * capacity + ranking


def slot_sources(destination, slot_count):
    positions = jnp.arange(slot_count, dtype=jnp.int32)
    matches = destination[None, :] == positions[:, None]
    block_numbers = jnp.arange(destination.shape[0], dtype=jnp.int32)
    source = jnp.sum(jnp.where(matches, block_numbers[None, :], 0), axis=1)
    return (source, jnp.any(matches, axis=1))


def match_tiles(arrived_tiles, tile_count):
    tile_numbers = jnp.arange(tile_count, dtype=jnp.float32)
    return (arrived_tiles[None, :] == tile_numbers[:, None]).astype(jnp.float32)


def update_grid(deposits, tile_match, cell_drag):
    tile_count = tile_match.shape[0]
    flattened = deposits.reshape(deposits.shape[0], -1)
    summed = jnp.dot(tile_match, flattened, preferred_element_type=jnp.float32)
    summed = summed.reshape((tile_count,) + deposits.shape[1:])
    grid_velocity = summed[:, 1:] / (summed[:, :1] + cell_drag[:, None, :])
    rounded = grid_velocity.astype(jnp.bfloat16)
    picked = jnp.dot(
        tile_match.T.astype(jnp.bfloat16),
        rounded.reshape(tile_count, -1),
        preferred_element_type=jnp.float32,
    )
    cell_rows = picked.astype(jnp.bfloat16).reshape((deposits.shape[0], 3, -1))
    return (grid_velocity, cell_rows)


def per_device(
    particle_mass,
    particle_velocity,
    particle_affine,
    particle_cell,
    particle_fraction,
    block_owner,
    block_slot,
    block_count,
    cell_drag,
):
    group_size = lax.axis_size(("gy", "gz"))
    blocks = block_count.shape[0]
    capacity = max(1, 2 * blocks // group_size)
    slot_count = group_size * capacity
    tile_count = cell_drag.shape[0]
    particle_data = particle_table(
        particle_mass,
        particle_velocity,
        particle_affine,
        particle_cell,
        particle_fraction,
        block_count,
    )
    destination = send_slots(block_owner[:, 0], group_size, capacity)
    source, filled = slot_sources(destination, slot_count)
    tile_ids = jnp.where(filled, jnp.take(block_slot, source), -1).astype(jnp.float32)
    deposits = deposit_all(particle_data)
    outgoing = jnp.where(filled[:, None, None], jnp.take(deposits, source, axis=0), 0.0)
    arrived, arrived_tiles = (
        lax.all_to_all(outgoing, ("gy", "gz"), split_axis=0, concat_axis=0, tiled=True),
        lax.all_to_all(tile_ids, ("gy", "gz"), split_axis=0, concat_axis=0, tiled=True),
    )
    tile_match = match_tiles(arrived_tiles, tile_count)
    grid_velocity, cell_rows = update_grid(arrived, tile_match, cell_drag)
    returned = lax.all_to_all(cell_rows, ("gy", "gz"), split_axis=0, concat_axis=0, tiled=True)
    finished = interpolate_all(particle_data, jnp.take(returned, destination, axis=0))
    new_velocity = finished[:3].reshape(3, -1)
    new_affine = finished[3:].reshape(9, -1)
    return (grid_velocity, new_velocity, new_affine)


def solution(mesh):
    return jax.shard_map(
        per_device,
        mesh=mesh,
        in_specs=(
            P(("gx", "gy", "gz")),
            P(None, ("gx", "gy", "gz")),
            P(None, ("gx", "gy", "gz")),
            P(None, ("gx", "gy", "gz")),
            P(None, ("gx", "gy", "gz")),
            P(("gx", "gy", "gz"), None),
            P(("gx", "gy", "gz")),
            P(("gx", "gy", "gz")),
            P(("gx", "gy", "gz"), None),
        ),
        out_specs=(
            P(("gx", "gy", "gz"), None, None),
            P(None, ("gx", "gy", "gz")),
            P(None, ("gx", "gy", "gz")),
        ),
        check_vma=False,
    )
```

profile of v0, /device:TPU:24, one launch (start us, length us, event | category | flops | bytes accessed | tf_op | source)
XLA Modules:
  0.0 570.1 jit_solution(11761494286336790737)
XLA Ops:
  5.7 11.5 %all-to-all-start = ((f32[32,4,1]{1,2,0:T(1,128)}), f32[32,4,1]{1,2,0:T(1,128)S(1)}, u32[]{:S(2)}, u32[]{:S(2)}) async-start(f32[32,4,1]{1,2,0:T(1,128)} %copy.85), calls=%async_computation | async-start | bytes 32768 | tf_op jit(solution)/shard_map/all_to_all | solution.py:217
  17.2 2.8 copy.92
  23.5 167.7 %while.23 = (s32[]{:T(128)}, bf16[16,4,4,4096]{3,2,1,0:T(4,128)(2,1)}, s32[16]{0:T(128)S(1)}, f32[16,64,512]{2,1,0:T(8,128)}, s32[]{:T(128)}, /*index=5*/s32[]{:...) while((s32[]{:T(128)}, bf16[16,4,4,4096]{3,2,1,0:T(4,128)(2,1)}, s32[16]{0:T(128)S(1)}, ...), condition=%wide.region_5.6_spmd, body=%wide.region_4.5_spmd.sunk | while | flops 173600768 | bytes 15057635 | solution.py:126
  191.2 9.1 %gather_fusion.1 = bf16[128,4,4096]{2,1,0:T(4,128)(2,1)} fusion(bf16[64,4,4096]{2,1,0:T(4,128)(2,1)} %bitcast.212, s32[1024]{0:T(1024)S(1)} %pad_clamp_fusion.1), kind=kCustom, calls=%fused_computation.1 | custom fusion | bytes 8389120 | tf_op jit(solution)/shard_map/jit(_take)/gather | solution.py:214
  200.3 7.1 %select_select_fusion = bf16[128,4,4096]{2,1,0:T(4,128)(2,1)} fusion(bf16[128,4,4096]{2,1,0:T(4,128)(2,1)} %gather_fusion.1, pred[128]{0:T(512)(128)(4,1)S(1)} %compare_and_fusion, pred[128]{0:T(512)(128)(4,1)S(1)} %fusion.22), kind=kLoop, calls=%fused_computation.72 | loop fusion | flops 4194304 | bytes 8388864 | tf_op jit(solution)/shard_map/jit(_where)/select_n | solution.py:214
  207.3 9.8 %all-to-all-start.1 = ((bf16[128,4,4096]{2,1,0:T(4,128)(2,1)}), bf16[128,4,4096]{2,1,0:T(4,128)(2,1)}, u32[]{:S(2)}, u32[]{:S(2)}) async-start(bf16[128,4,4096]{2,1,0:T(4,128)(2,1)} %select_select_fusion), calls=%async_computation.1 | async-start | bytes 8388608 | tf_op jit(solution)/shard_map/all_to_all | solution.py:216
  218.5 91.6 %all-to-all-done.1 = bf16[128,4,4096]{2,1,0:T(4,128)(2,1)} async-done(((bf16[128,4,4096]{2,1,0:T(4,128)(2,1)}), bf16[128,4,4096]{2,1,0:T(4,128)(2,1)}, u32[]{:S(2)}, u32[]{:S(2)}) %all-to-all-start.1) | async-done | bytes 4194336 | tf_op jit(solution)/shard_map/all_to_all | solution.py:216
  310.1 7.9 %copy.86 = bf16[128,4,4096]{0,2,1:T(8,128)(2,1)} copy(bf16[128,4,4096]{2,1,0:T(4,128)(2,1)} %all-to-all-done.1) | data formatting | bytes 8388608 | tf_op jit(solution)/shard_map/all_to_all | solution.py:216
  318.0 3.4 fusion.17
  322.5 2.7 convolution_convert_fusion
  325.1 3.5 copy.88
  328.6 5.5 copy.89
  334.1 7.6 %all-to-all-start.2 = ((bf16[128,3,4096]{2,1,0:T(4,128)(2,1)}), bf16[128,3,4096]{2,1,0:T(4,128)(2,1)}, u32[]{:S(2)}, u32[]{:S(2)}) async-start(bf16[128,3,4096]{2,1,0:T(4,128)(2,1)} %copy.89), calls=%async_computation.2 | async-start | bytes 8388608 | tf_op jit(solution)/shard_map/all_to_all | solution.py:221
  341.8 95.4 %all-to-all-done.2 = bf16[128,3,4096]{2,1,0:T(4,128)(2,1)} async-done(((bf16[128,3,4096]{2,1,0:T(4,128)(2,1)}), bf16[128,3,4096]{2,1,0:T(4,128)(2,1)}, u32[]{:S(2)}, u32[]{:S(2)}) %all-to-all-start.2) | async-done | bytes 3145760 | tf_op jit(solution)/shard_map/all_to_all | solution.py:221
  437.2 4.5 gather_fusion.2
  441.8 2.4 broadcast_select_fusion
  445.5 118.2 %while.24 = (s32[]{:T(128)}, f32[12,64,512]{2,1,0:T(8,128)}, f32[16,64,512]{2,1,0:T(8,128)}, bf16[64,3,4096]{2,1,0:T(4,128)(2,1)}, s32[]{:T(128)}, /*index=5*/s32[]{:T(128)}, s32[]{:T(128)}, s32[]{:T(128)}, s32[]{}) while((s32[]{:T(128)}, f32[12,64,512]{2,1,0:T(8,128)}, f32[16,64,512]{2,1,0:T(8,128)}, bf16[64,3,4096]{2,1,0:T(4,128)(2,1)}, ...), condition=%wide.region_11.12_spmd, body=%wide.region_6.11_spmd.sunk | while | flops 156190720 | bytes 13369515 | solution.py:146
  447.5 1.6 constant_dynamic-slice_fusion.11
  454.9 1.6 constant_dynamic-slice_fusion.11
  462.2 1.6 constant_dynamic-slice_fusion.11
  469.6 1.6 constant_dynamic-slice_fusion.11
  477.0 1.6 constant_dynamic-slice_fusion.11
  484.4 1.6 constant_dynamic-slice_fusion.11
  491.8 1.6 constant_dynamic-slice_fusion.11
  499.2 1.6 constant_dynamic-slice_fusion.11
  506.5 1.6 constant_dynamic-slice_fusion.11
  513.9 1.6 constant_dynamic-slice_fusion.11
  521.3 1.6 constant_dynamic-slice_fusion.11
  528.7 1.6 constant_dynamic-slice_fusion.11
  543.5 1.6 constant_dynamic-slice_fusion.11
  558.3 1.6 constant_dynamic-slice_fusion.11
  566.5 2.5 copy.95
  (732 shorter events, 265.4 us)
Async XLA Ops:
  0.6 2.7 copy-start
  5.7 201.6 %all-to-all-start = ((f32[32,4,1]{1,2,0:T(1,128)}), f32[32,4,1]{1,2,0:T(1,128)S(1)}, u32[]{:S(2)}, u32[]{:S(2)}) async-start(f32[32,4,1]{1,2,0:T(1,128)} %copy.85), calls=%async_computation | async-start | bytes 32768 | tf_op jit(solution)/shard_map/all_to_all | solution.py:217
  20.1 0.9 copy-start.6
  20.1 1.1 copy-start.2
  20.1 1.3 copy-start.3
  20.1 1.5 copy-start.4
  21.0 0.8 copy-start.8
  207.3 102.8 %all-to-all-start.1 = ((bf16[128,4,4096]{2,1,0:T(4,128)(2,1)}), bf16[128,4,4096]{2,1,0:T(4,128)(2,1)}, u32[]{:S(2)}, u32[]{:S(2)}) async-start(bf16[128,4,4096]{2,1,0:T(4,128)(2,1)} %select_select_fusion), calls=%async_computation.1 | async-start | bytes 8388608 | tf_op jit(solution)/shard_map/all_to_all | solution.py:216
  318.0 3.4 copy-start.5
  334.1 7.6 %copy-start.7 = (s32[64,1]{0,1:T(1,128)S(1)}, s32[64,1]{0,1:T(1,128)}, u32[]{:S(2)}) copy-start(s32[64,1]{0,1:T(1,128)} %param.18) | copy-start | bytes 772
  334.1 103.1 %all-to-all-start.2 = ((bf16[128,3,4096]{2,1,0:T(4,128)(2,1)}), bf16[128,3,4096]{2,1,0:T(4,128)(2,1)}, u32[]{:S(2)}, u32[]{:S(2)}) async-start(bf16[128,3,4096]{2,1,0:T(4,128)(2,1)} %copy.89), calls=%async_computation.2 | async-start | bytes 8388608 | tf_op jit(solution)/shard_map/all_to_all | solution.py:221
  566.5 3.6 copy-start.1
where the time goes:
time: 576 us; the launch traced here: 570 us
  waiting for transfers between devices  187 us (32%)
  local copies, waits for them, and re-layouts  160 us (28%)
  other arithmetic  109 us (19%)
  matrix products  70.1 us (12%)
  starting transfers between devices  28.9 us (5%)
  loops' own time  13.9 us (2%)
    all_to_all x1, waiting for transfers between devices, per_device(): lax.all_to_all(cell_rows, ('gy', 'gz'), split_axis=0, concat_axis=0, tile...  95.4 us
    all_to_all x1, waiting for transfers between devices, per_device(): lax.all_to_all(outgoing, ('gy', 'gz'), split_axis=0, concat_axis=0, tiled...  91.6 us
    dot_general x48, matrix products, contract(): jnp.einsum('anp,bnp->nab', flattened, plane, preferred_element_type=jnp.f...  50.1 us
    convert_element_type x32, other arithmetic, outer(): product_table.reshape((EDGE * EDGE,) + product_table.shape[2:])  29 us
    dynamic_slice x16, local copies, waits for them, and re-layouts, interpolate_advance(): lax.dynamic_slice_in_dim(grid_rows, first_block, batch_blocks, 0)  25.8 us
    reshape x16, local copies, waits for them, and re-layouts, interpolate(): flattened = grid_rows.reshape(batch_shape[0], 3 * EDGE, EDGE * EDGE)  16.8 us
    slice x16, local copies, waits for them, and re-layouts, deposit(): affine = particle_data[4:13].reshape((3, 3) + batch_shape)  14.9 us
    another operation x32, other arithmetic  14.9 us
  transfers between devices with their start and end apart: 3, of which 2 were waited for; matrix products, arithmetic and copies ran while one was open for 31% of the time, Pallas kernels for 0%

commit v1 on v0

v1 whole, which is shorter than its diff:
```python
import functools

import jax
import jax.numpy as jnp
from jax import lax
from jax.experimental import pallas as pl
from jax.experimental.pallas import tpu as pltpu
from jax.sharding import PartitionSpec as P

EDGE = 16
PLANE = EDGE * EDGE
QUANT = 1024
LANES = 128
ROWS = 80
BACK = 48
CENTER = 7.5
SMEM = pltpu.SMEM
VMEM = pltpu.VMEM


def pack_kernel(
    owner_ref, tile_ref, mass_ref, vel_ref, aff_ref, cell_ref, frac_ref, out_ref, dest_ref, used_ref, scratch, *, capacity, group
):
    blocks = dest_ref.shape[0]
    length = vel_ref.shape[1] // blocks
    parts = length // LANES

    def clear(owner, carry):
        used_ref[owner] = 0
        for rank in range(capacity):
            first = pl.multiple_of((owner * capacity + rank) * ROWS, 16)
            out_ref[pl.ds(first, 16), :] = jnp.full((16, LANES), -1.0, jnp.bfloat16)
        return carry

    lax.fori_loop(0, group, clear, 0)

    def place(block):
        owner = owner_ref[block]
        rank = used_ref[owner]
        used_ref[owner] = rank + 1
        slot = owner * capacity + rank
        dest_ref[block] = slot
        return slot

    def move(block, slot, buffer):
        where = pl.ds(pl.multiple_of(block * length, LANES), length)
        code = cell_ref[:, where] * QUANT + frac_ref[:, where]
        high = code >> 7
        low = (code & 127).astype(jnp.float32)
        buffer[0:9, :] = aff_ref[:, where]
        buffer[9:12, :] = vel_ref[:, where]
        buffer[12:15, :] = high.astype(jnp.float32)
        buffer[15:16, :] = jnp.full((1, length), tile_ref[block], jnp.int32).astype(jnp.float32)
        first = pl.multiple_of(slot * ROWS, 16)
        packed = buffer[...].astype(jnp.bfloat16)
        for part in range(parts):
            out_ref[pl.ds(pl.multiple_of(first + 16 * part, 16), 16), :] = packed[:, part * LANES : (part + 1) * LANES]
        pieces = [low[e : e + 1, part * LANES : (part + 1) * LANES] for e in range(3) for part in range(parts)]
        pieces.append(mass_ref[block])
        aux = jnp.concatenate(pieces, axis=0)
        out_ref[pl.ds(pl.multiple_of(first + 16 * parts, 16), 16), :] = aux.astype(jnp.bfloat16)

    def step(index, carry):
        slots = [place(index * 2 + k) for k in range(2)]
        for k in range(2):
            move(index * 2 + k, slots[k], scratch.at[k])
        return carry

    lax.fori_loop(0, blocks // 2, step, 0)


def node_weights(position):
    nodes = lax.broadcasted_iota(jnp.int32, (EDGE, position.shape[1]), 0).astype(jnp.float32)
    offset = nodes - position
    outer = jnp.maximum(1.5 - jnp.abs(offset), 0.0)
    inner = jnp.maximum(outer - 1.0, 0.0)
    return 0.5 * outer * outer - 1.5 * inner * inner, offset


def split(value):
    high = value.astype(jnp.bfloat16)
    return high, (value - high.astype(jnp.float32)).astype(jnp.bfloat16)


def particle_rows(data_ref, slot, parts):
    first = pl.multiple_of(slot * ROWS, 16)
    main = jnp.concatenate(
        [data_ref[pl.ds(pl.multiple_of(first + 16 * part, 16), 16), :] for part in range(parts)], axis=1
    ).astype(jnp.float32)
    aux = data_ref[pl.ds(pl.multiple_of(first + 16 * parts, 16), 16), :].astype(jnp.float32)

    def spread(row):
        return jnp.concatenate([aux[row * parts + part : row * parts + part + 1] for part in range(parts)], axis=1)

    positions = [main[12 + e : 13 + e] * 0.125 + (spread(e) * (1.0 / QUANT) + (0.5 + 0.5 / QUANT)) for e in range(3)]
    return main, spread(3), positions


def plane_table(weight_y, weight_z):
    return jnp.concatenate([(weight_y[y : y + 1] * weight_z).astype(jnp.bfloat16) for y in range(EDGE)], axis=0)


def deposit_block(data_ref, slot, parts):
    main, mass, (pos_x, pos_y, pos_z) = particle_rows(data_ref, slot, parts)
    weight_x, offset_x = node_weights(pos_x)
    weight_y, unused = node_weights(pos_y)
    weight_z, unused = node_weights(pos_z)
    plane = plane_table(weight_y, weight_z)
    center_y = pos_y - CENTER
    center_z = pos_z - CENTER
    loaded = mass * weight_x
    exact = [[], [], []]
    for d in range(3):
        column_zero, column_one, column_two = (main[3 * d + e : 3 * d + e + 1] for e in range(3))
        base = main[9 + d : 10 + d] - column_one * center_y - column_two * center_z
        exact[0].append(loaded * (base + column_zero * offset_x))
        exact[1].append(loaded * column_one)
        exact[2].append(loaded * column_two)
    halves = [split(value) for rows in exact for value in rows]
    lead = jnp.concatenate(
        [loaded.astype(jnp.bfloat16)] + [high for high, low in halves] + [low for high, low in halves], axis=0
    )
    sums = lax.dot_general(lead, plane, (((1,), (1,)), ((), ())), preferred_element_type=jnp.float32)
    momentum = sums[EDGE : 10 * EDGE] + sums[10 * EDGE :]
    return jnp.concatenate([sums[:EDGE], momentum], axis=0)


def interpolate_block(data_ref, grid_rows, slot, parts):
    unused, unused, (pos_x, pos_y, pos_z) = particle_rows(data_ref, slot, parts)
    weight_x, offset_x = node_weights(pos_x)
    weight_y, unused = node_weights(pos_y)
    weight_z, unused = node_weights(pos_z)
    plane = plane_table(weight_y, weight_z)
    moments = jnp.dot(grid_rows, plane, preferred_element_type=jnp.float32)
    span = 3 * EDGE
    moment_zero = moments[:span]
    moment_one = moments[span : 2 * span] + moments[2 * span : 3 * span]
    moment_two = moments[3 * span : 4 * span] + moments[4 * span :]
    center_y = pos_y - CENTER
    center_z = pos_z - CENTER

    def total(value):
        return jnp.sum(value, axis=0, keepdims=True)

    velocity, affine = [], []
    for d in range(3):
        rows = slice(d * EDGE, (d + 1) * EDGE)
        weighted = weight_x * moment_zero[rows]
        speed = total(weighted)
        velocity.append(speed)
        affine.append(4.0 * total(weighted * offset_x))
        affine.append(4.0 * (total(weight_x * moment_one[rows]) - center_y * speed))
        affine.append(4.0 * (total(weight_x * moment_two[rows]) - center_z * speed))
    return affine + velocity


def main_kernel(
    tile_ref, data_ref, drag_ref, back_ref, grid_ref, list_ref, sums_ref, rows_ref, scratch, *, parts
):
    slots = tile_ref.shape[0]
    tiles = drag_ref.shape[0]

    def collect(slot, count):
        @pl.when(tile_ref[slot] >= 0)
        def _():
            list_ref[count] = slot

        return count + (tile_ref[slot] >= 0).astype(jnp.int32)

    count = lax.fori_loop(0, slots, collect, 0)
    pairs = (count + 1) // 2

    def clear(tile, carry):
        sums_ref[tile] = jnp.zeros(sums_ref.shape[1:], jnp.float32)
        return carry

    lax.fori_loop(0, tiles, clear, 0)

    def second_of(pair):
        return list_ref[jnp.minimum(2 * pair + 1, count - 1)]

    def deposit_pair(pair, carry):
        first = list_ref[2 * pair]
        second = second_of(pair)
        spare = jnp.where(2 * pair + 1 < count, tile_ref[second], tiles)
        one = deposit_block(data_ref, first, parts)
        two = deposit_block(data_ref, second, parts)
        tile = tile_ref[first]
        sums_ref[tile] = sums_ref[tile] + one
        sums_ref[spare] = sums_ref[spare] + two
        return carry

    lax.fori_loop(0, pairs, deposit_pair, 0)

    lane = lax.broadcasted_iota(jnp.int32, (EDGE, PLANE), 1)
    node_y = (lane >> 4).astype(jnp.float32) - CENTER
    node_z = (lane & 15).astype(jnp.float32) - CENTER

    def update(tile, carry):
        sums = sums_ref[tile]
        weight = sums[:EDGE] + drag_ref[tile]
        ones, twos, zeros = [], [], []
        for d in range(3):
            zero, one, two = (sums[EDGE * (1 + 3 * e + d) : EDGE * (2 + 3 * e + d)] for e in range(3))
            speed = (zero + node_y * one + node_z * two) / weight
            grid_ref[tile, d] = speed
            rounded = speed.astype(jnp.bfloat16)
            zeros.append(rounded)
            ones.append(split(rounded.astype(jnp.float32) * node_y))
            twos.append(split(rounded.astype(jnp.float32) * node_z))
        rows = zeros + [high for high, low in ones] + [low for high, low in ones]
        rows = rows + [high for high, low in twos] + [low for high, low in twos]
        rows_ref[tile] = jnp.concatenate(rows, axis=0)
        return carry

    lax.fori_loop(0, tiles, update, 0)

    def send(values, slot, buffer):
        for row, value in enumerate(values):
            for part in range(parts):
                at = part * 8 + row if row < 8 else 8 * parts + part * 4 + row - 8
                buffer[at : at + 1, :] = value[:, part * LANES : (part + 1) * LANES]
        back_ref[pl.ds(pl.multiple_of(slot * BACK, 16), BACK), :] = buffer[...].astype(jnp.bfloat16)

    def interpolate_pair(pair, carry):
        first = list_ref[2 * pair]
        second = second_of(pair)
        one = interpolate_block(data_ref, rows_ref[tile_ref[first]], first, parts)
        two = interpolate_block(data_ref, rows_ref[tile_ref[second]], second, parts)
        send(one, first, scratch.at[0])
        send(two, second, scratch.at[1])
        return carry

    lax.fori_loop(0, pairs, interpolate_pair, 0)


def unpack_kernel(dest_ref, count_ref, back_ref, vel_ref, aff_ref):
    blocks = dest_ref.shape[0]
    length = vel_ref.shape[1] // blocks
    parts = length // LANES

    def one(block):
        first = pl.multiple_of(dest_ref[block] * BACK, 16)
        rows = back_ref[pl.ds(first, BACK), :].astype(jnp.float32)
        for part in range(parts):
            lane = lax.broadcasted_iota(jnp.int32, (8, LANES), 1) + part * LANES
            present = lane < count_ref[block]
            where = pl.ds(pl.multiple_of(block * length + part * LANES, LANES), LANES)
            aff_ref[0:8, where] = jnp.where(present, rows[part * 8 : part * 8 + 8], 0.0)
            rest = jnp.where(present[:4], rows[8 * parts + part * 4 : 8 * parts + part * 4 + 4], 0.0)
            aff_ref[8:9, where] = rest[0:1]
            vel_ref[:, where] = rest[1:4]

    def step(index, carry):
        for k in range(2):
            one(index * 2 + k)
        return carry

    lax.fori_loop(0, blocks // 2, step, 0)


def per_device(
    particle_mass,
    particle_velocity,
    particle_affine,
    particle_cell,
    particle_fraction,
    block_owner,
    block_slot,
    block_count,
    cell_drag,
):
    group = lax.axis_size(("gy", "gz"))
    blocks = block_count.shape[0]
    particles = particle_mass.shape[0]
    capacity = max(1, 2 * blocks // group)
    slots = group * capacity
    tiles = cell_drag.shape[0]
    length = particles // blocks
    parts = length // LANES
    mass = particle_mass.reshape(blocks, parts, LANES)
    live = lax.broadcasted_iota(jnp.int32, mass.shape, 1) * LANES + lax.broadcasted_iota(jnp.int32, mass.shape, 2)
    mass = jnp.where(live < block_count[:, None, None], mass, 0.0)
    smem = pl.BlockSpec(memory_space=SMEM)
    vmem = pl.BlockSpec(memory_space=VMEM)
    outgoing, destination = pl.pallas_call(
        functools.partial(pack_kernel, capacity=capacity, group=group),
        out_shape=(
            jax.ShapeDtypeStruct((slots * ROWS, LANES), jnp.bfloat16),
            jax.ShapeDtypeStruct((blocks,), jnp.int32),
        ),
        in_specs=[smem, smem, vmem, vmem, vmem, vmem, vmem],
        out_specs=(vmem, smem),
        scratch_shapes=[SMEM((group,), jnp.int32), VMEM((2, 16, length), jnp.float32)],
        name="pack",
    )(block_owner.reshape(blocks), block_slot, mass, particle_velocity, particle_affine, particle_cell, particle_fraction)
    arrived = lax.all_to_all(outgoing, ("gy", "gz"), split_axis=0, concat_axis=0, tiled=True)
    tile_ids = arrived.reshape(slots, ROWS, LANES)[:, 15, 0].astype(jnp.int32)
    span = 3 * EDGE
    back, grid = pl.pallas_call(
        functools.partial(main_kernel, parts=parts),
        out_shape=(
            jax.ShapeDtypeStruct((slots * BACK, LANES), jnp.bfloat16),
            jax.ShapeDtypeStruct((tiles, 3, EDGE, PLANE), jnp.float32),
        ),
        in_specs=[smem, vmem, vmem],
        out_specs=(vmem, vmem),
        scratch_shapes=[
            SMEM((slots,), jnp.int32),
            VMEM((tiles + 1, 10 * EDGE, PLANE), jnp.float32),
            VMEM((tiles, 5 * span, PLANE), jnp.bfloat16),
            VMEM((2, BACK, LANES), jnp.float32),
        ],
        name="transfer",
    )(tile_ids, arrived, cell_drag.reshape(tiles, EDGE, PLANE))
    returned = lax.all_to_all(back, ("gy", "gz"), split_axis=0, concat_axis=0, tiled=True)
    new_velocity, new_affine = pl.pallas_call(
        unpack_kernel,
        out_shape=(
            jax.ShapeDtypeStruct((3, particles), jnp.float32),
            jax.ShapeDtypeStruct((9, particles), jnp.float32),
        ),
        in_specs=[smem, smem, vmem],
        out_specs=(vmem, vmem),
        name="unpack",
    )(destination, block_count, returned)
    return (grid.reshape(tiles, 3, EDGE * PLANE), new_velocity, new_affine)


def solution(mesh):
    whole = ("gx", "gy", "gz")
    return jax.shard_map(
        per_device,
        mesh=mesh,
        in_specs=(
            P(whole),
            P(None, whole),
            P(None, whole),
            P(None, whole),
            P(None, whole),
            P(whole, None),
            P(whole),
            P(whole),
            P(whole, None),
        ),
        out_specs=(P(whole, None, None), P(None, whole), P(None, whole)),
        check_vma=False,
    )
```

time: 576 us -> 192 us (0.33)
  local copies, waits for them, and re-layouts: 160 us -> 3.03 us
  other arithmetic: 109 us -> 4.66 us
  waiting for transfers between devices: 187 us -> 94.7 us
  matrix products: 70.1 us -> 0 us
  Pallas kernels: 0 us -> 53.7 us
  loops' own time: 13.9 us -> 0 us
    dot_general x98 -> x0, matrix products: 70.1 us -> none  [the longest x48 50.1 us: contract(): jnp.einsum('anp,bnp->nab', flattened, plane, preferred_element_type=jnp.f...]
    all_to_all x2 -> x1, waiting for transfers between devices: 95.4 us -> 35 us  [per_device(): lax.all_to_all(back, ('gy', 'gz'), split_axis=0, concat_axis=0, tiled=True)]
    pallas_call x0 -> x3, Pallas kernels: none -> 53.7 us  [the longest x1 45 us: per_device(): pl.pallas_call(functools.partial(main_kernel, parts=parts), out_shape=(ja...]
    slice x97 -> x0, local copies, waits for them, and re-layouts: 43.9 us -> none  [the longest x16 14.9 us: deposit(): affine = particle_data[4:13].reshape((3, 3) + batch_shape)]
    dynamic_slice x32 -> x0, local copies, waits for them, and re-layouts: 35.1 us -> none  [the longest x16 25.8 us: interpolate_advance(): lax.dynamic_slice_in_dim(grid_rows, first_block, batch_blocks, 0)]
    all_to_all x1, waiting for transfers between devices: 91.6 us -> 59.7 us  [per_device(): lax.all_to_all(outgoing, ('gy', 'gz'), split_axis=0, concat_axis=0, tiled...]
    reshape x69 -> x1, local copies, waits for them, and re-layouts: 28.2 us -> 1.02 us  [per_device(): return (grid.reshape(tiles, 3, EDGE * PLANE), new_velocity, new_affine)]
    convert_element_type x34 -> x1, other arithmetic: 29.8 us -> 2.95 us  [per_device(): tile_ids = arrived.reshape(slots, ROWS, LANES)[:, 15, 0].astype(jnp.int32)]
  transfers between devices with their start and end apart: 3 -> 2, of which waited for: 2 -> 2; matrix products, arithmetic and copies ran while one was open for 31% -> 1% of each run, Pallas kernels for 0% -> 0%
where the time goes in v1:
time: 192 us; the launch traced here: 191 us
  waiting for transfers between devices  94.7 us (49%)
  Pallas kernels  53.7 us (28%)
  starting transfers between devices  34.2 us (18%)
  other arithmetic  4.66 us (2%)
  local copies, waits for them, and re-layouts  3.03 us (2%)
    all_to_all x1, waiting for transfers between devices, per_device(): lax.all_to_all(outgoing, ('gy', 'gz'), split_axis=0, concat_axis=0, tiled...  59.7 us
    pallas_call x1, Pallas kernels, per_device(): pl.pallas_call(functools.partial(main_kernel, parts=parts), out_shape=(ja...  45 us
    all_to_all x1, waiting for transfers between devices, per_device(): lax.all_to_all(back, ('gy', 'gz'), split_axis=0, concat_axis=0, tiled=True)  35 us
    all_to_all x1, starting transfers between devices, per_device(): lax.all_to_all(back, ('gy', 'gz'), split_axis=0, concat_axis=0, tiled=True)  22.6 us
    all_to_all x1, starting transfers between devices, per_device(): lax.all_to_all(outgoing, ('gy', 'gz'), split_axis=0, concat_axis=0, tiled...  11.6 us
    pallas_call x1, Pallas kernels, per_device(): pl.pallas_call(functools.partial(pack_kernel, capacity=capacity, group=gr...  5.02 us
  transfers between devices with their start and end apart: 2, of which 2 were waited for; matrix products, arithmetic and copies ran while one was open for 1% of the time, Pallas kernels for 0%

profile of v1, /device:TPU:24, one launch (start us, length us, event | category | flops | bytes accessed | tf_op | source)
XLA Modules:
  0.0 191.0 jit_solution(13511400347615534774)
XLA Ops:
  0.6 1.7 fusion.mass_ref
  2.3 5.0 %pack.1 = (bf16[10240,128]{1,0:T(8,128)(2,1)}, s32[64]{0:T(128)}) custom-call(s32[64]{0:T(128)} %bitcast.21, s32[64]{0:T(128)} %tile_ref.1, f32[64,4,128]{2,1,0:T(4,128)} %fusion.mass_ref, f32[3,32768]{1,0:T(4,128)} %vel_ref.1, f32[9,32768]{1,0:T(8,128)} %aff_ref.1, s32[3,32768]{1,0:T(4,128)} %cell_ref.1, s32[3,32768]{1,0:T(4,128)} %frac_ref.1), custom_call_target="tpu_custom_call" | custom-call | tf_op jit(solution)/shard_map/pack/pallas_call | solution.py:286
  7.4 0.0 copy-start.3
  7.4 11.6 %all-to-all-start = ((bf16[32,320,128]{2,1,0:T(8,128)(2,1)}), bf16[32,320,128]{2,1,0:T(8,128)(2,1)S(1)}, u32[]{:S(2)}, u32[]{:S(2)}) async-start(bf16[32,320,128]{2,1,0:T(8,128)(2,1)} %bitcast.16), calls=%async_computation | async-start | bytes 5242880 | tf_op jit(solution)/shard_map/all_to_all | solution.py:297
  19.0 0.0 copy-done.3
  19.0 0.8 copy.15
  19.8 59.7 %all-to-all-done = bf16[32,320,128]{2,1,0:T(8,128)(2,1)S(1)} async-done(((bf16[32,320,128]{2,1,0:T(8,128)(2,1)}), bf16[32,320,128]{2,1,0:T(8,128)(2,1)S(1)}, u32[]{:S(2)}, u32[]{:S(2)}) %all-to-all-start) | async-done | bytes 2621472 | tf_op jit(solution)/shard_map/all_to_all | solution.py:297
  79.5 0.0 copy-start
  79.5 3.0 %fusion.1.tile_ref = s32[128]{0:T(128)} fusion(bf16[128,80,128]{2,1,0:T(8,128)(2,1)S(1)} %bitcast.13), kind=kLoop, calls=%fused_computation.3 | loop fusion | flops 128 | bytes 768 | tf_op jit(solution)/shard_map/convert_element_type | solution.py:298
  82.4 0.0 copy-done
  82.4 45.0 %transfer.1 = (bf16[6144,128]{1,0:T(8,128)(2,1)}, f32[16,3,16,256]{3,2,1,0:T(8,128)}) custom-call(s32[128]{0:T(128)} %fusion.1.tile_ref, bf16[10240,128]{1,0:T(8,128)(2,1)} %bitcast.14, f32[16,16,256]{2,1,0:T(8,128)} %bitcast.18), custom_call_target="tpu_custom_call" | custom-call | tf_op jit(solution)/shard_map/transfer/pallas_call | solution.py:300
  127.5 0.0 copy-start.2
  127.5 22.6 %all-to-all-start.1 = ((bf16[32,192,128]{2,1,0:T(8,128)(2,1)}), bf16[32,192,128]{2,1,0:T(8,128)(2,1)S(1)}, u32[]{:S(2)}, u32[]{:S(2)}) async-start(bf16[32,192,128]{2,1,0:T(8,128)(2,1)} %bitcast.17), calls=%async_computation.1 | async-start | bytes 3145728 | tf_op jit(solution)/shard_map/all_to_all | solution.py:316
  150.0 0.0 copy-done.2
  150.1 0.1 copy.14
  150.1 1.0 reshape.33
  151.1 35.0 %all-to-all-done.1 = bf16[32,192,128]{2,1,0:T(8,128)(2,1)S(1)} async-done(((bf16[32,192,128]{2,1,0:T(8,128)(2,1)}), bf16[32,192,128]{2,1,0:T(8,128)(2,1)S(1)}, u32[]{:S(2)}, u32[]{:S(2)}) %all-to-all-start.1) | async-done | bytes 1572896 | tf_op jit(solution)/shard_map/all_to_all | solution.py:316
  186.2 0.0 copy-start.1
  186.2 1.1 copy-done.1
  187.3 3.7 %unpack.1 = (f32[3,32768]{1,0:T(4,128)}, f32[9,32768]{1,0:T(8,128)}) custom-call(s32[64]{0:T(128)} %get-tuple-element.11.dest_ref, s32[64]{0:T(128)} %count_ref.1, bf16[6144,128]{1,0:T(8,128)(2,1)} %bitcast.15), custom_call_target="tpu_custom_call" | custom-call | tf_op jit(solution)/shard_map/unpack/pallas_call | solution.py:317
  (1 shorter events, 0.0 us)
Async XLA Ops:
  7.4 11.6 %copy-start.3 = (f32[16,4096]{1,0:T(8,128)S(1)}, f32[16,4096]{1,0:T(8,128)}, u32[]{:S(2)}) copy-start(f32[16,4096]{1,0:T(8,128)} %param.17) | copy-start | bytes 786436
  7.4 72.1 %all-to-all-start = ((bf16[32,320,128]{2,1,0:T(8,128)(2,1)}), bf16[32,320,128]{2,1,0:T(8,128)(2,1)S(1)}, u32[]{:S(2)}, u32[]{:S(2)}) async-start(bf16[32,320,128]{2,1,0:T(8,128)(2,1)} %bitcast.16), calls=%async_computation | async-start | bytes 5242880 | tf_op jit(solution)/shard_map/all_to_all | solution.py:297
  79.5 3.0 %copy-start = (bf16[32,320,128]{2,1,0:T(8,128)(2,1)}, bf16[32,320,128]{2,1,0:T(8,128)(2,1)S(1)}, u32[]{:S(2)}) copy-start(bf16[32,320,128]{2,1,0:T(8,128)(2,1)S(1)} %all-to-all-done) | copy-start | bytes 7864324
  127.5 22.6 %copy-start.2 = (f32[16,3,16,256]{3,2,1,0:T(8,128)S(1)}, f32[16,3,16,256]{3,2,1,0:T(8,128)}, u32[]{:S(2)}) copy-start(f32[16,3,16,256]{3,2,1,0:T(8,128)} %get-tuple-element.10) | copy-start | bytes 2359300
  127.5 58.7 %all-to-all-start.1 = ((bf16[32,192,128]{2,1,0:T(8,128)(2,1)}), bf16[32,192,128]{2,1,0:T(8,128)(2,1)S(1)}, u32[]{:S(2)}, u32[]{:S(2)}) async-start(bf16[32,192,128]{2,1,0:T(8,128)(2,1)} %bitcast.17), calls=%async_computation.1 | async-start | bytes 3145728 | tf_op jit(solution)/shard_map/all_to_all | solution.py:316
  186.2 1.1 copy-start.1

commit v2 on v1

--- a/solution.py
+++ b/solution.py
@@ -19,16 +19,34 @@
 
 
 def pack_kernel(
-    owner_ref, tile_ref, mass_ref, vel_ref, aff_ref, cell_ref, frac_ref, out_ref, dest_ref, used_ref, scratch, *, capacity, group
+    owner_ref,
+    tile_ref,
+    count_ref,
+    mass_ref,
+    vel_ref,
+    aff_ref,
+    cell_ref,
+    frac_ref,
+    out_ref,
+    dest_ref,
+    used_ref,
+    scratch,
+    *,
+    capacity,
+    group,
 ):
+    half = capacity // 2
     blocks = dest_ref.shape[0]
     length = vel_ref.shape[1] // blocks
     parts = length // LANES
 
+    def slot_of(owner, rank):
+        return (rank // half) * (group * half) + owner * half + rank % half
+
     def clear(owner, carry):
         used_ref[owner] = 0
         for rank in range(capacity):
-            first = pl.multiple_of((owner * capacity + rank) * ROWS, 16)
+            first = pl.multiple_of(slot_of(owner, rank) * ROWS, 16)
             out_ref[pl.ds(first, 16), :] = jnp.full((16, LANES), -1.0, jnp.bfloat16)
         return carry
 
@@ -38,7 +56,7 @@
         owner = owner_ref[block]
         rank = used_ref[owner]
         used_ref[owner] = rank + 1
-        slot = owner * capacity + rank
+        slot = slot_of(owner, rank)
         dest_ref[block] = slot
         return slot
 
@@ -56,7 +74,9 @@
         for part in range(parts):
             out_ref[pl.ds(pl.multiple_of(first + 16 * part, 16), 16), :] = packed[:, part * LANES : (part + 1) * LANES]
         pieces = [low[e : e + 1, part * LANES : (part + 1) * LANES] for e in range(3) for part in range(parts)]
-        pieces.append(mass_ref[block])
+        place_in_block = lax.broadcasted_iota(jnp.int32, (parts, LANES), 0) * LANES
+        place_in_block = place_in_block + lax.broadcasted_iota(jnp.int32, (parts, LANES), 1)
+        pieces.append(jnp.where(place_in_block < count_ref[block], mass_ref[block], 0.0))
         aux = jnp.concatenate(pieces, axis=0)
         out_ref[pl.ds(pl.multiple_of(first + 16 * parts, 16), 16), :] = aux.astype(jnp.bfloat16)
 
@@ -154,44 +174,87 @@
     return affine + velocity
 
 
-def main_kernel(
-    tile_ref, data_ref, drag_ref, back_ref, grid_ref, list_ref, sums_ref, rows_ref, scratch, *, parts
-):
-    slots = tile_ref.shape[0]
-    tiles = drag_ref.shape[0]
+def arrivals(data_ref, row_ref, tile_ref, list_ref, sem):
+    slots = row_ref.shape[0]
+
+    def read(slot, carry):
+        first = data_ref[pl.ds(pl.multiple_of(slot * ROWS, 16), 16), :].astype(jnp.float32)
+        row_ref[pl.ds(slot, 1), :] = first[15:16].astype(jnp.int32)
+        return carry
+
+    lax.fori_loop(0, slots, read, 0, unroll=4)
+    copy = pltpu.make_async_copy(row_ref, tile_ref, sem)
+    copy.start()
+    copy.wait()
 
     def collect(slot, count):
-        @pl.when(tile_ref[slot] >= 0)
+        filled = tile_ref[slot, 0] >= 0
+
+        @pl.when(filled)
         def _():
             list_ref[count] = slot
 
-        return count + (tile_ref[slot] >= 0).astype(jnp.int32)
-
-    count = lax.fori_loop(0, slots, collect, 0)
-    pairs = (count + 1) // 2
+        return count + filled.astype(jnp.int32)
+
+    return lax.fori_loop(0, slots, collect, 0)
+
+
+def pair_of(pair, count, list_ref, tile_ref, spare):
+    first = list_ref[2 * pair]
+    second = list_ref[jnp.minimum(2 * pair + 1, count - 1)]
+    other = jnp.where(2 * pair + 1 < count, tile_ref[second, 0], spare)
+    return first, second, tile_ref[first, 0], other
+
+
+def deposit_all(data_ref, sums_ref, tile_ref, list_ref, count, parts):
+    spare = sums_ref.shape[0] - 1
+
+    def step(pair, carry):
+        first, second, tile, other = pair_of(pair, count, list_ref, tile_ref, spare)
+        one = deposit_block(data_ref, first, parts)
+        two = deposit_block(data_ref, second, parts)
+        sums_ref[tile] = sums_ref[tile] + one
+        sums_ref[other] = sums_ref[other] + two
+        return carry
+
+    lax.fori_loop(0, (count + 1) // 2, step, 0)
+
+
+def interpolate_all(data_ref, rows_ref, back_ref, scratch, tile_ref, list_ref, count, parts):
+    def send(values, slot, buffer):
+        for row, value in enumerate(values):
+            for part in range(parts):
+                at = part * 8 + row if row < 8 else 8 * parts + part * 4 + row - 8
+                buffer[at : at + 1, :] = value[:, part * LANES : (part + 1) * LANES]
+        back_ref[pl.ds(pl.multiple_of(slot * BACK, 16), BACK), :] = buffer[...].astype(jnp.bfloat16)
+
+    def step(pair, carry):
+        first, second, tile, unused = pair_of(pair, count, list_ref, tile_ref, 0)
+        one = interpolate_block(data_ref, rows_ref[tile], first, parts)
+        two = interpolate_block(data_ref, rows_ref[tile_ref[second, 0]], second, parts)
+        send(one, first, scratch.at[0])
+        send(two, second, scratch.at[1])
+        return carry
+
+    lax.fori_loop(0, (count + 1) // 2, step, 0)
+
+
+def early_kernel(data_ref, sums_ref, row_ref, tile_ref, list_ref, sem, *, parts):
+    count = arrivals(data_ref, row_ref, tile_ref, list_ref, sem)
 
     def clear(tile, carry):
         sums_ref[tile] = jnp.zeros(sums_ref.shape[1:], jnp.float32)
         return carry
 
-    lax.fori_loop(0, tiles, clear, 0)
-
-    def second_of(pair):
-        return list_ref[jnp.minimum(2 * pair + 1, count - 1)]
-
-    def deposit_pair(pair, carry):
-        first = list_ref[2 * pair]
-        second = second_of(pair)
-        spare = jnp.where(2 * pair + 1 < count, tile_ref[second], tiles)
-        one = deposit_block(data_ref, first, parts)
-        two = deposit_block(data_ref, second, parts)
-        tile = tile_ref[first]
-        sums_ref[tile] = sums_ref[tile] + one
-        sums_ref[spare] = sums_ref[spare] + two
-        return carry
-
-    lax.fori_loop(0, pairs, deposit_pair, 0)
-
+    lax.fori_loop(0, sums_ref.shape[0], clear, 0)
+    deposit_all(data_ref, sums_ref, tile_ref, list_ref, count, parts)
+
+
+def middle_kernel(
+    early_ref, late_ref, sums_ref, drag_ref, back_ref, grid_ref, rows_ref, row_ref, tile_ref, list_ref, scratch, sem, *, parts
+):
+    count = arrivals(late_ref, row_ref, tile_ref, list_ref, sem)
+    deposit_all(late_ref, sums_ref, tile_ref, list_ref, count, parts)
     lane = lax.broadcasted_iota(jnp.int32, (EDGE, PLANE), 1)
     node_y = (lane >> 4).astype(jnp.float32) - CENTER
     node_z = (lane & 15).astype(jnp.float32) - CENTER
@@ -213,35 +276,24 @@
         rows_ref[tile] = jnp.concatenate(rows, axis=0)
         return carry
 
-    lax.fori_loop(0, tiles, update, 0)
-
-    def send(values, slot, buffer):
-        for row, value in enumerate(values):
-            for part in range(parts):
-                at = part * 8 + row if row < 8 else 8 * parts + part * 4 + row - 8
-                buffer[at : at + 1, :] = value[:, part * LANES : (part + 1) * LANES]
-        back_ref[pl.ds(pl.multiple_of(slot * BACK, 16), BACK), :] = buffer[...].astype(jnp.bfloat16)
-
-    def interpolate_pair(pair, carry):
-        first = list_ref[2 * pair]
-        second = second_of(pair)
-        one = interpolate_block(data_ref, rows_ref[tile_ref[first]], first, parts)
-        two = interpolate_block(data_ref, rows_ref[tile_ref[second]], second, parts)
-        send(one, first, scratch.at[0])
-        send(two, second, scratch.at[1])
-        return carry
-
-    lax.fori_loop(0, pairs, interpolate_pair, 0)
-
-
-def unpack_kernel(dest_ref, count_ref, back_ref, vel_ref, aff_ref):
+    lax.fori_loop(0, drag_ref.shape[0], update, 0)
+    count = arrivals(early_ref, row_ref, tile_ref, list_ref, sem)
+    interpolate_all(early_ref, rows_ref, back_ref, scratch, tile_ref, list_ref, count, parts)
+
+
+def last_kernel(data_ref, rows_ref, back_ref, row_ref, tile_ref, list_ref, scratch, sem, *, parts):
+    count = arrivals(data_ref, row_ref, tile_ref, list_ref, sem)
+    interpolate_all(data_ref, rows_ref, back_ref, scratch, tile_ref, list_ref, count, parts)
+
+
+def unpack_kernel(dest_ref, count_ref, early_ref, late_ref, vel_ref, aff_ref):
     blocks = dest_ref.shape[0]
     length = vel_ref.shape[1] // blocks
     parts = length // LANES
-
-    def one(block):
-        first = pl.multiple_of(dest_ref[block] * BACK, 16)
-        rows = back_ref[pl.ds(first, BACK), :].astype(jnp.float32)
+    half = early_ref.shape[0] // BACK
+
+    def put(block, source, slot):
+        rows = source[pl.ds(pl.multiple_of(slot * BACK, 16), BACK), :].astype(jnp.float32)
         for part in range(parts):
             lane = lax.broadcasted_iota(jnp.int32, (8, LANES), 1) + part * LANES
             present = lane < count_ref[block]
@@ -251,12 +303,20 @@
             aff_ref[8:9, where] = rest[0:1]
             vel_ref[:, where] = rest[1:4]
 
-    def step(index, carry):
-        for k in range(2):
-            one(index * 2 + k)
-        return carry
-
-    lax.fori_loop(0, blocks // 2, step, 0)
+    def step(block, carry):
+        slot = dest_ref[block]
+
+        @pl.when(slot < half)
+        def _():
+            put(block, early_ref, slot)
+
+        @pl.when(slot >= half)
+        def _():
+            put(block, late_ref, slot - half)
+
+        return carry
+
+    lax.fori_loop(0, blocks, step, 0)
 
 
 def per_device(
@@ -278,9 +338,7 @@
     tiles = cell_drag.shape[0]
     length = particles // blocks
     parts = length // LANES
-    mass = particle_mass.reshape(blocks, parts, LANES)
-    live = lax.broadcasted_iota(jnp.int32, mass.shape, 1) * LANES + lax.broadcasted_iota(jnp.int32, mass.shape, 2)
-    mass = jnp.where(live < block_count[:, None, None], mass, 0.0)
+    half = slots // 2
     smem = pl.BlockSpec(memory_space=SMEM)
     vmem = pl.BlockSpec(memory_space=VMEM)
     outgoing, destination = pl.pallas_call(
@@ -289,41 +347,68 @@
             jax.ShapeDtypeStruct((slots * ROWS, LANES), jnp.bfloat16),
             jax.ShapeDtypeStruct((blocks,), jnp.int32),
         ),
-        in_specs=[smem, smem, vmem, vmem, vmem, vmem, vmem],
+        in_specs=[smem, smem, smem, vmem, vmem, vmem, vmem, vmem],
         out_specs=(vmem, smem),
         scratch_shapes=[SMEM((group,), jnp.int32), VMEM((2, 16, length), jnp.float32)],
         name="pack",
-    )(block_owner.reshape(blocks), block_slot, mass, particle_velocity, particle_affine, particle_cell, particle_fraction)
-    arrived = lax.all_to_all(outgoing, ("gy", "gz"), split_axis=0, concat_axis=0, tiled=True)
-    tile_ids = arrived.reshape(slots, ROWS, LANES)[:, 15, 0].astype(jnp.int32)
+    )(
+        block_owner.reshape(blocks),
+        block_slot,
+        block_count,
+        particle_mass.reshape(blocks, parts, LANES),
+        particle_velocity,
+        particle_affine,
+        particle_cell,
+        particle_fraction,
+    )
+
+    def exchange(array):
+        return lax.all_to_all(array, ("gy", "gz"), split_axis=0, concat_axis=0, tiled=True)
+
+    early = exchange(outgoing[: half * ROWS])
+    late = exchange(outgoing[half * ROWS :])
     span = 3 * EDGE
-    back, grid = pl.pallas_call(
-        functools.partial(main_kernel, parts=parts),
-        out_shape=(
-            jax.ShapeDtypeStruct((slots * BACK, LANES), jnp.bfloat16),
-            jax.ShapeDtypeStruct((tiles, 3, EDGE, PLANE), jnp.float32),
-        ),
-        in_specs=[smem, vmem, vmem],
-        out_specs=(vmem, vmem),
-        scratch_shapes=[
-            SMEM((slots,), jnp.int32),
-            VMEM((tiles + 1, 10 * EDGE, PLANE), jnp.float32),
-            VMEM((tiles, 5 * span, PLANE), jnp.bfloat16),
-            VMEM((2, BACK, LANES), jnp.float32),
-        ],
-        name="transfer",
-    )(tile_ids, arrived, cell_drag.reshape(tiles, EDGE, PLANE))
-    returned = lax.all_to_all(back, ("gy", "gz"), split_axis=0, concat_axis=0, tiled=True)
+    back_shape = jax.ShapeDtypeStruct((half * BACK, LANES), jnp.bfloat16)
+    rows_shape = jax.ShapeDtypeStruct((tiles, 5 * span, PLANE), jnp.bfloat16)
+    listing = [VMEM((half, LANES), jnp.int32), SMEM((half, LANES), jnp.int32), SMEM((half,), jnp.int32)]
+    buffers = VMEM((2, BACK, LANES), jnp.float32)
+    done = pltpu.SemaphoreType.DMA
+    sums = pl.pallas_call(
+        functools.partial(early_kernel, parts=parts),
+        out_shape=jax.ShapeDtypeStruct((tiles + 1, 10 * EDGE, PLANE), jnp.float32),
+        in_specs=[vmem],
+        out_specs=vmem,
+        scratch_shapes=listing + [done],
+        name="early",
+    )(early)
+    back_early, grid, rows = pl.pallas_call(
+        functools.partial(middle_kernel, parts=parts),
+        out_shape=(back_shape, jax.ShapeDtypeStruct((tiles, 3, EDGE, PLANE), jnp.float32), rows_shape),
+        in_specs=[vmem, vmem, vmem, vmem],
+        out_specs=(vmem, vmem, vmem),
+        scratch_shapes=listing + [buffers, done],
+        name="middle",
+    )(early, late, sums, cell_drag.reshape(tiles, EDGE, PLANE))
+    returned_early = exchange(back_early)
+    back_late = pl.pallas_call(
+        functools.partial(last_kernel, parts=parts),
+        out_shape=back_shape,
+        in_specs=[vmem, vmem],
+        out_specs=vmem,
+        scratch_shapes=listing + [buffers, done],
+        name="last",
+    )(late, rows)
+    returned_late = exchange(back_late)
     new_velocity, new_affine = pl.pallas_call(
         unpack_kernel,
         out_shape=(
             jax.ShapeDtypeStruct((3, particles), jnp.float32),
             jax.ShapeDtypeStruct((9, particles), jnp.float32),
         ),
-        in_specs=[smem, smem, vmem],
+        in_specs=[smem, smem, vmem, vmem],
         out_specs=(vmem, vmem),
         name="unpack",
-    )(destination, block_count, returned)
+    )(destination, block_count, returned_early, returned_late)
     return (grid.reshape(tiles, 3, EDGE * PLANE), new_velocity, new_affine)
 
 

time: 192 us -> 188 us (0.979)
  blocking collectives: 0 us -> 45 us
  waiting for transfers between devices: 94.7 us -> 54 us
  Pallas kernels: 53.7 us -> 42.5 us
  other arithmetic: 4.66 us -> 0 us
  local copies, waits for them, and re-layouts: 3.03 us -> 6.8 us
  starting transfers between devices: 34.2 us -> 36.6 us
    all_to_all x0 -> x1, blocking collectives: none -> 45 us  [exchange(): lax.all_to_all(array, ('gy', 'gz'), split_axis=0, concat_axis=0, tiled=True)]
    all_to_all x2 -> x3, waiting for transfers between devices: 94.7 us -> 54 us  [exchange(): lax.all_to_all(array, ('gy', 'gz'), split_axis=0, concat_axis=0, tiled=True)]
    pallas_call x1 -> x3, Pallas kernels: 45 us -> 32.6 us  [the longest x1 15.1 us: per_device(): pl.pallas_call(functools.partial(middle_kernel, parts=parts), out_shape=(...]
    convert_element_type x1 -> x0, other arithmetic: 2.95 us -> none  [per_device(): tile_ids = arrived.reshape(slots, ROWS, LANES)[:, 15, 0].astype(jnp.int32)]
    slice x0 -> x1, local copies, waits for them, and re-layouts: none -> 2.94 us  [per_device(): late = exchange(outgoing[half * ROWS:])]
    all_to_all x2 -> x3, starting transfers between devices: 34.2 us -> 36.6 us  [exchange(): lax.all_to_all(array, ('gy', 'gz'), split_axis=0, concat_axis=0, tiled=True)]
  transfers between devices with their start and end apart: 2 -> 3, of which waited for: 2 -> 3; matrix products, arithmetic and copies ran while one was open for 1% -> 1% of each run, Pallas kernels for 0% -> 9%
where the time goes in v2:
time: 188 us; the launch traced here: 186 us
  waiting for transfers between devices  54 us (29%)
  blocking collectives  45 us (24%)
  Pallas kernels  42.5 us (23%)
  starting transfers between devices  36.6 us (19%)
  local copies, waits for them, and re-layouts  6.8 us (4%)
    all_to_all x3, waiting for transfers between devices, exchange(): lax.all_to_all(array, ('gy', 'gz'), split_axis=0, concat_axis=0, tiled=True)  54 us
    all_to_all x1, blocking collectives, exchange(): lax.all_to_all(array, ('gy', 'gz'), split_axis=0, concat_axis=0, tiled=True)  45 us
    all_to_all x3, starting transfers between devices, exchange(): lax.all_to_all(array, ('gy', 'gz'), split_axis=0, concat_axis=0, tiled=True)  36.6 us
    pallas_call x1, Pallas kernels, per_device(): pl.pallas_call(functools.partial(middle_kernel, parts=parts), out_shape=(...  15.1 us
    pallas_call x1, Pallas kernels, per_device(): pl.pallas_call(functools.partial(early_kernel, parts=parts), out_shape=ja...  12.7 us
    pallas_call x1, Pallas kernels, per_device(): pl.pallas_call(functools.partial(pack_kernel, capacity=capacity, group=gr...  5.37 us
    pallas_call x1, Pallas kernels, per_device(): pl.pallas_call(functools.partial(last_kernel, parts=parts), out_shape=bac...  4.83 us
    pallas_call x1, Pallas kernels, per_device(): pl.pallas_call(unpack_kernel, out_shape=(jax.ShapeDtypeStruct((3, particl...  4.52 us
  transfers between devices with their start and end apart: 3, of which 3 were waited for; matrix products, arithmetic and copies ran while one was open for 1% of the time, Pallas kernels for 9%

profile of v2, /device:TPU:24, one launch (start us, length us, event | category | flops | bytes accessed | tf_op | source)
XLA Modules:
  0.0 185.7 jit_solution(11266549910570380024)
XLA Ops:
  0.6 5.4 %pack.1 = (bf16[10240,128]{1,0:T(8,128)(2,1)}, s32[64]{0:T(128)}) custom-call(s32[64]{0:T(128)} %bitcast.28, s32[64]{0:T(128)} %tile_ref.1, s32[64]{0:T(128)} %count_ref.3, f32[64,4,128]{2,1,0:T(4,128)} %bitcast.27, f32[3,32768]{1,0:T(4,128)} %vel_ref.1, f32[9,32768]{1,0:T(8,128)} %aff_ref.1, s32[3,32768]{1,0:T(4,128)} %cell_ref.1, s32[3,32768]{1,0:T(4,128)} %frac_ref.1), custom_call_target="tpu_custom_call" | custom-call | tf_op jit(solution)/shard_map/pack/pallas_call | solution.py:344
  6.0 2.9 %fusion = (bf16[5120,128]{1,0:T(8,128)(2,1)}, bf16[5120,128]{1,0:T(8,128)(2,1)S(1)}) fusion(bf16[10240,128]{1,0:T(8,128)(2,1)} %get-tuple-element.10), kind=kLoop, calls=%fused_computation | loop fusion | bytes 5242880 | tf_op jit(solution)/shard_map/slice | solution.py:369
  8.9 45.0 %all_to_all.44 = bf16[32,160,128]{2,1,0:T(8,128)(2,1)} all-to-all(bf16[32,160,128]{2,1,0:T(8,128)(2,1)S(1)} %bitcast.20), channel_id=1, replica_groups=mesh['gx'=8,'gy'=8,'gz'=4] {'gy','gz'}, dimensions={0} | all-to-all | bytes 2621440 | tf_op jit(solution)/shard_map/all_to_all | solution.py:366
  54.0 0.0 copy-start.4
  54.0 5.7 %all-to-all-start.1 = ((bf16[32,160,128]{2,1,0:T(8,128)(2,1)}), bf16[32,160,128]{2,1,0:T(8,128)(2,1)S(1)}, u32[]{:S(2)}, u32[]{:S(2)}) async-start(bf16[32,160,128]{2,1,0:T(8,128)(2,1)} %bitcast.4), calls=%async_computation.1 | async-start | bytes 2621440 | tf_op jit(solution)/shard_map/all_to_all | solution.py:366
  59.7 0.0 copy-done.4
  59.7 0.8 copy.14
  60.5 12.7 %early.1.sums_ref = f32[17,160,256]{2,1,0:T(8,128)} custom-call(bf16[5120,128]{1,0:T(8,128)(2,1)} %bitcast.18), custom_call_target="tpu_custom_call" | custom-call | tf_op jit(solution)/shard_map/early/pallas_call | solution.py:376
  73.2 19.3 %all-to-all-done.1 = bf16[32,160,128]{2,1,0:T(8,128)(2,1)S(1)} async-done(((bf16[32,160,128]{2,1,0:T(8,128)(2,1)}), bf16[32,160,128]{2,1,0:T(8,128)(2,1)S(1)}, u32[]{:S(2)}, u32[]{:S(2)}) %all-to-all-start.1) | async-done | bytes 1310752 | tf_op jit(solution)/shard_map/all_to_all | solution.py:366
  92.5 0.0 copy-start
  92.5 1.1 copy-done
  93.6 15.1 %middle.1 = (bf16[3072,128]{1,0:T(8,128)(2,1)}, f32[16,3,16,256]{3,2,1,0:T(8,128)}, bf16[16,240,256]{2,1,0:T(8,128)(2,1)}) custom-call(bf16[5120,128]{1,0:T(8,128)(2,1)} %bitcast.19, bf16[5120,128]{1,0:T(8,128)(2,1)} %bitcast.16, f32[17,160,256]{2,1,0:T(8,128)} %early.1.sums_ref, f32[16,16,256]{2,1,0:T(8,128)} %bitcast.24), custom_call_target="tpu_custom_call" | custom-call | tf_op jit(solution)/shard_map/middle/pallas_call | solution.py:384
  108.6 25.3 %all-to-all-start.2 = ((bf16[32,96,128]{2,1,0:T(8,128)(2,1)}), bf16[32,96,128]{2,1,0:T(8,128)(2,1)S(1)}, u32[]{:S(2)}, u32[]{:S(2)}) async-start(bf16[32,96,128]{2,1,0:T(8,128)(2,1)} %bitcast.25), calls=%async_computation.2 | async-start | bytes 1572864 | tf_op jit(solution)/shard_map/all_to_all | solution.py:366
  133.9 0.0 copy-start.3
  134.0 4.8 %last.1 = bf16[3072,128]{1,0:T(8,128)(2,1)} custom-call(bf16[5120,128]{1,0:T(8,128)(2,1)} %bitcast.17, bf16[16,240,256]{2,1,0:T(8,128)(2,1)} %get-tuple-element.14.rows_ref), custom_call_target="tpu_custom_call" | custom-call | tf_op jit(solution)/shard_map/last/pallas_call | solution.py:393
  138.8 15.8 %all-to-all-done.2 = bf16[32,96,128]{2,1,0:T(8,128)(2,1)S(1)} async-done(((bf16[32,96,128]{2,1,0:T(8,128)(2,1)}), bf16[32,96,128]{2,1,0:T(8,128)(2,1)S(1)}, u32[]{:S(2)}, u32[]{:S(2)}) %all-to-all-start.2) | async-done | bytes 786464 | tf_op jit(solution)/shard_map/all_to_all | solution.py:366
  154.6 0.0 copy-start.1
  154.6 5.6 %all-to-all-start.3 = ((bf16[32,96,128]{2,1,0:T(8,128)(2,1)}), bf16[32,96,128]{2,1,0:T(8,128)(2,1)S(1)}, u32[]{:S(2)}, u32[]{:S(2)}) async-start(bf16[32,96,128]{2,1,0:T(8,128)(2,1)} %bitcast.23), calls=%async_computation.3 | async-start | bytes 1572864 | tf_op jit(solution)/shard_map/all_to_all | solution.py:366
  160.1 0.0 copy-done.3
  160.1 0.1 copy.13
  160.2 1.0 reshape.29
  161.2 0.0 copy-done.1
  161.2 19.0 %all-to-all-done.3 = bf16[32,96,128]{2,1,0:T(8,128)(2,1)S(1)} async-done(((bf16[32,96,128]{2,1,0:T(8,128)(2,1)}), bf16[32,96,128]{2,1,0:T(8,128)(2,1)S(1)}, u32[]{:S(2)}, u32[]{:S(2)}) %all-to-all-start.3) | async-done | bytes 786464 | tf_op jit(solution)/shard_map/all_to_all | solution.py:366
  180.2 0.0 copy-start.2
  180.2 0.9 copy-done.2
  181.1 4.5 %unpack.1 = (f32[3,32768]{1,0:T(4,128)}, f32[9,32768]{1,0:T(8,128)}) custom-call(s32[64]{0:T(128)} %get-tuple-element.12.dest_ref, s32[64]{0:T(128)} %count_ref.3, bf16[3072,128]{1,0:T(8,128)(2,1)} %bitcast.21, bf16[3072,128]{1,0:T(8,128)(2,1)} %bitcast.22), custom_call_target="tpu_custom_call" | custom-call | tf_op jit(solution)/shard_map/unpack/pallas_call | solution.py:402
Async XLA Ops:
  54.0 5.7 %copy-start.4 = (f32[16,4096]{1,0:T(8,128)S(1)}, f32[16,4096]{1,0:T(8,128)}, u32[]{:S(2)}) copy-start(f32[16,4096]{1,0:T(8,128)} %param.17) | copy-start | bytes 786436
  54.0 38.5 %all-to-all-start.1 = ((bf16[32,160,128]{2,1,0:T(8,128)(2,1)}), bf16[32,160,128]{2,1,0:T(8,128)(2,1)S(1)}, u32[]{:S(2)}, u32[]{:S(2)}) async-start(bf16[32,160,128]{2,1,0:T(8,128)(2,1)} %bitcast.4), calls=%async_computation.1 | async-start | bytes 2621440 | tf_op jit(solution)/shard_map/all_to_all | solution.py:366
  92.5 1.1 copy-start
  108.6 45.9 %all-to-all-start.2 = ((bf16[32,96,128]{2,1,0:T(8,128)(2,1)}), bf16[32,96,128]{2,1,0:T(8,128)(2,1)S(1)}, u32[]{:S(2)}, u32[]{:S(2)}) async-start(bf16[32,96,128]{2,1,0:T(8,128)(2,1)} %bitcast.25), calls=%async_computation.2 | async-start | bytes 1572864 | tf_op jit(solution)/shard_map/all_to_all | solution.py:366
  133.9 26.2 %copy-start.3 = (f32[16,3,16,256]{3,2,1,0:T(8,128)S(1)}, f32[16,3,16,256]{3,2,1,0:T(8,128)}, u32[]{:S(2)}) copy-start(f32[16,3,16,256]{3,2,1,0:T(8,128)} %get-tuple-element.11) | copy-start | bytes 2359300
  154.6 6.7 %copy-start.1 = (bf16[32,96,128]{2,1,0:T(8,128)(2,1)}, bf16[32,96,128]{2,1,0:T(8,128)(2,1)S(1)}, u32[]{:S(2)}) copy-start(bf16[32,96,128]{2,1,0:T(8,128)(2,1)S(1)} %all-to-all-done.2) | copy-start | bytes 2359300
  154.6 25.7 %all-to-all-start.3 = ((bf16[32,96,128]{2,1,0:T(8,128)(2,1)}), bf16[32,96,128]{2,1,0:T(8,128)(2,1)S(1)}, u32[]{:S(2)}, u32[]{:S(2)}) async-start(bf16[32,96,128]{2,1,0:T(8,128)(2,1)} %bitcast.23), calls=%async_computation.3 | async-start | bytes 1572864 | tf_op jit(solution)/shard_map/all_to_all | solution.py:366
  180.2 0.9 copy-start.2

commit v3 on v1

v3 whole, which is shorter than its diff:
```python
import functools

import jax
import jax.numpy as jnp
from jax import lax
from jax.experimental import pallas as pl
from jax.experimental.pallas import tpu as pltpu
from jax.sharding import PartitionSpec as P

EDGE = 16
PLANE = EDGE * EDGE
QUANT = 1024
LANES = 128
ROWS = 80
BACK = 48
CENTER = 7.5
SMEM = pltpu.SMEM
VMEM = pltpu.VMEM


def pack_kernel(
    owner_ref, tile_ref, count_ref, mass_ref, vel_ref, aff_ref, cell_ref, frac_ref, out_ref, dest_ref, used_ref, scratch, low_ref, *, capacity, group
):
    blocks = dest_ref.shape[0]
    length = vel_ref.shape[1] // blocks
    parts = length // LANES

    def clear(owner, carry):
        used_ref[owner] = 0
        for rank in range(capacity):
            first = pl.multiple_of((owner * capacity + rank) * ROWS, 16)
            out_ref[pl.ds(first, 16), :] = jnp.full((16, LANES), -1.0, jnp.bfloat16)
        return carry

    lax.fori_loop(0, group, clear, 0)

    def place(block):
        owner = owner_ref[block]
        rank = used_ref[owner]
        used_ref[owner] = rank + 1
        slot = owner * capacity + rank
        dest_ref[block] = slot
        return slot

    place_in_block = lax.broadcasted_iota(jnp.int32, (parts, LANES), 0) * LANES
    place_in_block = place_in_block + lax.broadcasted_iota(jnp.int32, (parts, LANES), 1)

    def move(block, slot, buffer, lows):
        where = pl.ds(pl.multiple_of(block * length, LANES), length)
        code = cell_ref[:, where] * QUANT + frac_ref[:, where]
        low = (code & 127).astype(jnp.float32)
        for d in range(3):
            buffer[d : d + 1, :] = aff_ref[3 * d + 1 : 3 * d + 2, where]
            buffer[8 + d : 9 + d, :] = aff_ref[3 * d + 2 : 3 * d + 3, where]
            buffer[3 + 4 * d : 4 + 4 * d, :] = aff_ref[3 * d : 3 * d + 1, where]
        buffer[4:7, :] = vel_ref[:, where]
        buffer[12:15, :] = (code >> 7).astype(jnp.float32)
        buffer[15:16, :] = jnp.full((1, length), tile_ref[block], jnp.int32).astype(jnp.float32)
        live = jnp.where(place_in_block < count_ref[block], mass_ref[block], 0.0)
        for part in range(parts):
            lows[4 * part : 4 * part + 3, :] = low[:, part * LANES : (part + 1) * LANES]
            lows[4 * part + 3 : 4 * part + 4, :] = live[part : part + 1]
        first = pl.multiple_of(slot * ROWS, 16)
        packed = buffer[...].astype(jnp.bfloat16)
        for part in range(parts):
            out_ref[pl.ds(pl.multiple_of(first + 16 * part, 16), 16), :] = packed[:, part * LANES : (part + 1) * LANES]
        out_ref[pl.ds(pl.multiple_of(first + 16 * parts, 16), 16), :] = lows[...].astype(jnp.bfloat16)

    def step(index, carry):
        slots = [place(index * 2 + k) for k in range(2)]
        for k in range(2):
            move(index * 2 + k, slots[k], scratch.at[k], low_ref.at[k])
        return carry

    lax.fori_loop(0, blocks // 2, step, 0)


def split(value):
    high = value.astype(jnp.bfloat16)
    return high, (value - high.astype(jnp.float32)).astype(jnp.bfloat16)


def sublanes():
    return lax.broadcasted_iota(jnp.int32, (8, LANES), 0)


def spread(ref, row):
    return ref[pl.ds(row, 8, stride=0), :]


CELL, FIRST, SECOND, THIRD, MIDDLE, SIDE, NODES = (64 + 16 * k for k in range(7))
BASE = NODES + 64
TABLE = BASE + 32


def prepare(data_ref, slot, table, parts, deposit):
    first = pl.multiple_of(slot * ROWS, 16)
    side = data_ref[pl.ds(pl.multiple_of(first + 16 * parts, 16), 16), :].astype(jnp.float32)
    highs = []
    for part in range(parts):
        main = data_ref[pl.ds(pl.multiple_of(first + 16 * part, 16), 16), :].astype(jnp.float32)
        if deposit:
            table[16 * part : 16 * part + 16, :] = main
        highs.append(main[8:])
    upper = sublanes() < 4
    high = jnp.concatenate(
        [jnp.where(upper, pltpu.roll(highs[k], 4, 0), highs[k + 1]) for k in range(0, parts, 2)], axis=0
    )
    high = high * 0.125
    cell = jnp.floor(high)
    inside = (high - cell) + (side * (1.0 / QUANT) + 0.5 / QUANT)
    rest = 1.0 - inside
    table[CELL : CELL + 16, :] = cell
    table[FIRST : FIRST + 16, :] = rest * rest
    table[SECOND : SECOND + 16, :] = 1.0 + 2.0 * (inside * rest)
    table[THIRD : THIRD + 16, :] = inside * inside
    table[MIDDLE : MIDDLE + 16, :] = cell + inside + (0.5 - CENTER)
    if deposit:
        table[SIDE : SIDE + 16, :] = side * 0.125


def node_weights(table, part, e, nodes):
    row = 4 * part + e
    cell = spread(table, CELL + row)
    one, two, three = (spread(table, at + row) for at in (FIRST, SECOND, THIRD))
    return [
        jnp.where(cell == node, one, jnp.where(cell == node - 1.0, two, jnp.where(cell == node - 2.0, three, 0.0)))
        for node in nodes
    ]


def plane_table(table, part, nodes):
    for half, weight in enumerate(node_weights(table, part, 1, nodes)):
        table[NODES + 16 * part + 8 * half : NODES + 16 * part + 8 * half + 8, :] = weight
    upper, lower = node_weights(table, part, 2, nodes)
    rows = []
    for y in range(EDGE):
        weight = spread(table, NODES + 16 * part + y)
        rows.append(jnp.concatenate([weight * upper, weight * lower], axis=0).astype(jnp.bfloat16))
    return jnp.concatenate(rows, axis=0)


def node_rows():
    node = sublanes().astype(jnp.float32)
    return [node, node + 8.0]


def deposit_block(data_ref, slot, table, parts):
    prepare(data_ref, slot, table, parts, True)
    nodes = node_rows()
    leads, planes = [], []
    for part in range(parts):
        planes.append(plane_table(table, part, nodes))
        row = 4 * part
        weights = node_weights(table, part, 0, nodes)
        middle = spread(table, MIDDLE + row)
        offsets = [(node - CENTER) - middle for node in nodes]
        mass = spread(table, SIDE + row + 3)
        loaded = [mass * weight for weight in weights]
        top = table[16 * part : 16 * part + 8, :]
        bottom = table[16 * part + 8 : 16 * part + 16, :]
        base = pltpu.roll(top, 4, 0) - top * spread(table, MIDDLE + row + 1) - bottom * spread(table, MIDDLE + row + 2)
        table[BASE + 8 * part : BASE + 8 * part + 8, :] = base
        highs, lows = [jnp.concatenate(loaded, axis=0).astype(jnp.bfloat16)], []

        def add(values):
            high, low = split(jnp.concatenate(values, axis=0))
            highs.append(high)
            lows.append(low)

        for d in range(3):
            shift = spread(table, BASE + 8 * part + d)
            along_x = spread(table, 16 * part + 3 + 4 * d)
            add([load * (shift + along_x * offset) for load, offset in zip(loaded, offsets)])
        for at in (0, 8):
            for d in range(3):
                column = spread(table, 16 * part + at + d)
                add([load * column for load in loaded])
        leads.append(jnp.concatenate(highs + lows, axis=0))
    lead = jnp.concatenate(leads, axis=1)
    plane = jnp.concatenate(planes, axis=1)
    sums = lax.dot_general(lead, plane, (((1,), (1,)), ((), ())), preferred_element_type=jnp.float32)
    momentum = sums[EDGE : 10 * EDGE] + sums[10 * EDGE :]
    return jnp.concatenate([sums[:EDGE], momentum], axis=0)


def fold(values):
    row = sublanes()
    for shift in (1, 2, 4):
        if len(values) == 1:
            return values[0] + pltpu.roll(values[0], 8 - shift, 0)
        mine = (row & shift) == 0
        values = [
            jnp.where(mine, one, two) + pltpu.roll(jnp.where(mine, two, one), 8 - shift, 0)
            for one, two in zip(values[0::2], values[1::2])
        ]
    return values[0]


def interpolate_block(data_ref, grid_rows, slot, table, back_ref, parts):
    prepare(data_ref, slot, table, parts, False)
    nodes = node_rows()
    plane = jnp.concatenate([plane_table(table, part, nodes) for part in range(parts)], axis=1)
    moments = jnp.dot(grid_rows, plane, preferred_element_type=jnp.float32)
    span = 3 * EDGE
    row = sublanes()
    eights, fours = [], []
    for part in range(parts):
        weights = node_weights(table, part, 0, nodes)
        middle = spread(table, MIDDLE + 4 * part)
        offsets = [(node - CENTER) - middle for node in nodes]
        lanes = slice(part * LANES, (part + 1) * LANES)
        zero, one, two, speed = [], [], [], []
        for d in range(3):
            halves = [d * EDGE, d * EDGE + 8]
            loaded = [weight * moments[at : at + 8, lanes] for weight, at in zip(weights, halves)]
            speed.append(loaded[0] + loaded[1])
            zero.append(loaded[0] * offsets[0] + loaded[1] * offsets[1])
            for first, into in ((span, one), (3 * span, two)):
                pieces = [
                    weight * (moments[first + at : first + at + 8, lanes] + moments[first + span + at : first + span + at + 8, lanes])
                    for weight, at in zip(weights, halves)
                ]
                into.append(pieces[0] + pieces[1])
        eight = fold([zero[0], one[0], two[0], zero[1], one[1], two[1], zero[2], one[2]])
        four = fold([two[2]] + speed)
        table[BASE + 8 * part : BASE + 8 * part + 8, :] = four
        speeds = [spread(table, BASE + 8 * part + 1 + d) for d in range(3)]
        center_y = spread(table, MIDDLE + 4 * part + 1)
        center_z = spread(table, MIDDLE + 4 * part + 2)
        column = row % 3
        center = jnp.where(column == 1, center_y, jnp.where(column == 2, center_z, 0.0))
        speed = jnp.where(row < 3, speeds[0], jnp.where(row < 6, speeds[1], speeds[2]))
        eights.append(0.5 * (eight - center * speed))
        fours.append(jnp.where((row & 3) == 0, 0.5 * (four - center_z * speeds[2]), 0.125 * four))
    first = pl.multiple_of(slot * BACK, 16)
    upper = row < 4
    merged = [jnp.where(upper, fours[k], fours[k + 1]) for k in range(0, parts, 2)]
    back_ref[pl.ds(first, BACK), :] = jnp.concatenate(eights + merged, axis=0).astype(jnp.bfloat16)


def arrivals(data_ref, row_ref, tile_ref, list_ref, sem):
    slots = row_ref.shape[0]

    def read(slot, carry):
        first = data_ref[pl.ds(pl.multiple_of(slot * ROWS, 16), 16), :].astype(jnp.float32)
        row_ref[pl.ds(slot, 1), :] = first[15:16].astype(jnp.int32)
        return carry

    lax.fori_loop(0, slots, read, 0, unroll=4)
    copy = pltpu.make_async_copy(row_ref, tile_ref, sem)
    copy.start()
    copy.wait()

    def collect(slot, count):
        filled = tile_ref[slot, 0] >= 0

        @pl.when(filled)
        def _():
            list_ref[count] = slot

        return count + filled.astype(jnp.int32)

    return lax.fori_loop(0, slots, collect, 0)


def main_kernel(
    data_ref, drag_ref, back_ref, grid_ref, row_ref, tile_ref, list_ref, sums_ref, rows_ref, table, sem, *, parts
):
    tiles = drag_ref.shape[0]
    count = arrivals(data_ref, row_ref, tile_ref, list_ref, sem)
    pairs = (count + 1) // 2

    def clear(tile, carry):
        sums_ref[tile] = jnp.zeros(sums_ref.shape[1:], jnp.float32)
        return carry

    lax.fori_loop(0, tiles, clear, 0)

    def second_of(pair):
        return list_ref[jnp.minimum(2 * pair + 1, count - 1)]

    def deposit_pair(pair, carry):
        first = list_ref[2 * pair]
        second = second_of(pair)
        spare = jnp.where(2 * pair + 1 < count, tile_ref[second, 0], tiles)
        one = deposit_block(data_ref, first, table.at[0], parts)
        two = deposit_block(data_ref, second, table.at[1], parts)
        tile = tile_ref[first, 0]
        sums_ref[tile] = sums_ref[tile] + one
        sums_ref[spare] = sums_ref[spare] + two
        return carry

    lax.fori_loop(0, pairs, deposit_pair, 0)

    lane = lax.broadcasted_iota(jnp.int32, (EDGE, PLANE), 1)
    node_y = (lane >> 4).astype(jnp.float32) - CENTER
    node_z = (lane & 15).astype(jnp.float32) - CENTER

    def update(tile, carry):
        sums = sums_ref[tile]
        weight = sums[:EDGE] + drag_ref[tile]
        ones, twos, zeros = [], [], []
        for d in range(3):
            zero, one, two = (sums[EDGE * (1 + 3 * e + d) : EDGE * (2 + 3 * e + d)] for e in range(3))
            speed = (zero + node_y * one + node_z * two) / weight
            grid_ref[tile, d] = speed
            rounded = speed.astype(jnp.bfloat16)
            zeros.append(rounded)
            ones.append(split(rounded.astype(jnp.float32) * node_y))
            twos.append(split(rounded.astype(jnp.float32) * node_z))
        rows = zeros + [high for high, low in ones] + [low for high, low in ones]
        rows = rows + [high for high, low in twos] + [low for high, low in twos]
        rows_ref[tile] = jnp.concatenate(rows, axis=0)
        return carry

    lax.fori_loop(0, tiles, update, 0)

    def interpolate_pair(pair, carry):
        first = list_ref[2 * pair]
        second = second_of(pair)
        interpolate_block(data_ref, rows_ref[tile_ref[first, 0]], first, table.at[0], back_ref, parts)
        interpolate_block(data_ref, rows_ref[tile_ref[second, 0]], second, table.at[1], back_ref, parts)
        return carry

    lax.fori_loop(0, pairs, interpolate_pair, 0)


def unpack_kernel(dest_ref, count_ref, back_ref, vel_ref, aff_ref):
    blocks = dest_ref.shape[0]
    length = vel_ref.shape[1] // blocks
    parts = length // LANES

    def one(block):
        first = pl.multiple_of(dest_ref[block] * BACK, 16)
        rows = back_ref[pl.ds(first, BACK), :].astype(jnp.float32)
        for part in range(parts):
            lane = lax.broadcasted_iota(jnp.int32, (8, LANES), 1) + part * LANES
            present = lane < count_ref[block]
            where = pl.ds(pl.multiple_of(block * length + part * LANES, LANES), LANES)
            aff_ref[0:8, where] = jnp.where(present, rows[part * 8 : part * 8 + 8], 0.0)
            rest = jnp.where(present[:4], rows[8 * parts + part * 4 : 8 * parts + part * 4 + 4], 0.0)
            aff_ref[8:9, where] = rest[0:1]
            vel_ref[:, where] = rest[1:4]

    def step(index, carry):
        for k in range(2):
            one(index * 2 + k)
        return carry

    lax.fori_loop(0, blocks // 2, step, 0)


def per_device(
    particle_mass,
    particle_velocity,
    particle_affine,
    particle_cell,
    particle_fraction,
    block_owner,
    block_slot,
    block_count,
    cell_drag,
):
    group = lax.axis_size(("gy", "gz"))
    blocks = block_count.shape[0]
    particles = particle_mass.shape[0]
    capacity = max(1, 2 * blocks // group)
    slots = group * capacity
    tiles = cell_drag.shape[0]
    length = particles // blocks
    parts = length // LANES
    smem = pl.BlockSpec(memory_space=SMEM)
    vmem = pl.BlockSpec(memory_space=VMEM)
    outgoing, destination = pl.pallas_call(
        functools.partial(pack_kernel, capacity=capacity, group=group),
        out_shape=(
            jax.ShapeDtypeStruct((slots * ROWS, LANES), jnp.bfloat16),
            jax.ShapeDtypeStruct((blocks,), jnp.int32),
        ),
        in_specs=[smem, smem, smem, vmem, vmem, vmem, vmem, vmem],
        out_specs=(vmem, smem),
        scratch_shapes=[
            SMEM((group,), jnp.int32),
            VMEM((2, 16, length), jnp.float32),
            VMEM((2, 16, LANES), jnp.float32),
        ],
        name="pack",
    )(
        block_owner.reshape(blocks),
        block_slot,
        block_count,
        particle_mass.reshape(blocks, parts, LANES),
        particle_velocity,
        particle_affine,
        particle_cell,
        particle_fraction,
    )
    arrived = lax.all_to_all(outgoing, ("gy", "gz"), split_axis=0, concat_axis=0, tiled=True)
    span = 3 * EDGE
    back, grid = pl.pallas_call(
        functools.partial(main_kernel, parts=parts),
        out_shape=(
            jax.ShapeDtypeStruct((slots * BACK, LANES), jnp.bfloat16),
            jax.ShapeDtypeStruct((tiles, 3, EDGE, PLANE), jnp.float32),
        ),
        in_specs=[vmem, vmem],
        out_specs=(vmem, vmem),
        scratch_shapes=[
            VMEM((slots, LANES), jnp.int32),
            SMEM((slots, LANES), jnp.int32),
            SMEM((slots,), jnp.int32),
            VMEM((tiles + 1, 10 * EDGE, PLANE), jnp.float32),
            VMEM((tiles, 5 * span, PLANE), jnp.bfloat16),
            VMEM((2, TABLE, LANES), jnp.float32),
            pltpu.SemaphoreType.DMA,
        ],
        name="transfer",
    )(arrived, cell_drag.reshape(tiles, EDGE, PLANE))
    returned = lax.all_to_all(back, ("gy", "gz"), split_axis=0, concat_axis=0, tiled=True)
    new_velocity, new_affine = pl.pallas_call(
        unpack_kernel,
        out_shape=(
            jax.ShapeDtypeStruct((3, particles), jnp.float32),
            jax.ShapeDtypeStruct((9, particles), jnp.float32),
        ),
        in_specs=[smem, smem, vmem],
        out_specs=(vmem, vmem),
        name="unpack",
    )(destination, block_count, returned)
    return (grid.reshape(tiles, 3, EDGE * PLANE), new_velocity, new_affine)


def solution(mesh):
    whole = ("gx", "gy", "gz")
    return jax.shard_map(
        per_device,
        mesh=mesh,
        in_specs=(
            P(whole),
            P(None, whole),
            P(None, whole),
            P(None, whole),
            P(None, whole),
            P(whole, None),
            P(whole),
            P(whole),
            P(whole, None),
        ),
        out_specs=(P(whole, None, None), P(None, whole), P(None, whole)),
        check_vma=False,
    )
```

time: 192 us -> 189 us (0.984)
  Pallas kernels: 53.7 us -> 43 us
  starting transfers between devices: 34.2 us -> 43.6 us
  other arithmetic: 4.66 us -> 0 us
  waiting for transfers between devices: 94.7 us -> 98 us
    pallas_call x1, Pallas kernels: 45 us -> 34.1 us  [per_device(): pl.pallas_call(functools.partial(main_kernel, parts=parts), out_shape=(ja...]
    all_to_all x1, starting transfers between devices: 22.6 us -> 32 us  [per_device(): lax.all_to_all(back, ('gy', 'gz'), split_axis=0, concat_axis=0, tiled=True)]
    all_to_all x1, waiting for transfers between devices: 35 us -> 38.3 us  [per_device(): lax.all_to_all(back, ('gy', 'gz'), split_axis=0, concat_axis=0, tiled=True)]
    convert_element_type x1 -> x0, other arithmetic: 2.95 us -> none  [per_device(): tile_ids = arrived.reshape(slots, ROWS, LANES)[:, 15, 0].astype(jnp.int32)]
where the time goes in v3:
time: 189 us; the launch traced here: 190 us
  waiting for transfers between devices  98 us (52%)
  starting transfers between devices  43.6 us (23%)
  Pallas kernels  43 us (23%)
  local copies, waits for them, and re-layouts  4.55 us (2%)
    all_to_all x1, waiting for transfers between devices, per_device(): lax.all_to_all(outgoing, ('gy', 'gz'), split_axis=0, concat_axis=0, tiled...  59.7 us
    all_to_all x1, waiting for transfers between devices, per_device(): lax.all_to_all(back, ('gy', 'gz'), split_axis=0, concat_axis=0, tiled=True)  38.3 us
    pallas_call x1, Pallas kernels, per_device(): pl.pallas_call(functools.partial(main_kernel, parts=parts), out_shape=(ja...  34.1 us
    all_to_all x1, starting transfers between devices, per_device(): lax.all_to_all(back, ('gy', 'gz'), split_axis=0, concat_axis=0, tiled=True)  32 us
    all_to_all x1, starting transfers between devices, per_device(): lax.all_to_all(outgoing, ('gy', 'gz'), split_axis=0, concat_axis=0, tiled...  11.6 us
    pallas_call x1, Pallas kernels, per_device(): pl.pallas_call(functools.partial(pack_kernel, capacity=capacity, group=gr...  5.28 us
  transfers between devices with their start and end apart: 2, of which 2 were waited for; matrix products, arithmetic and copies ran while one was open for 1% of the time, Pallas kernels for 0%

profile of v3, /device:TPU:24, one launch (start us, length us, event | category | flops | bytes accessed | tf_op | source)
XLA Modules:
  0.0 189.8 jit_solution(3586271265365292728)
XLA Ops:
  0.6 5.3 %pack.1 = (bf16[10240,128]{1,0:T(8,128)(2,1)}, s32[64]{0:T(128)}) custom-call(s32[64]{0:T(128)} %bitcast.19, s32[64]{0:T(128)} %tile_ref.1, s32[64]{0:T(128)} %count_ref.3, f32[64,4,128]{2,1,0:T(4,128)} %bitcast.18, f32[3,32768]{1,0:T(4,128)} %vel_ref.1, f32[9,32768]{1,0:T(8,128)} %aff_ref.1, s32[3,32768]{1,0:T(4,128)} %cell_ref.1, s32[3,32768]{1,0:T(4,128)} %frac_ref.1), custom_call_target="tpu_custom_call" | custom-call | tf_op jit(solution)/shard_map/pack/pallas_call | solution.py:375
  5.9 0.0 copy-start.3
  5.9 11.6 %all-to-all-start = ((bf16[32,320,128]{2,1,0:T(8,128)(2,1)}), bf16[32,320,128]{2,1,0:T(8,128)(2,1)S(1)}, u32[]{:S(2)}, u32[]{:S(2)}) async-start(bf16[32,320,128]{2,1,0:T(8,128)(2,1)} %bitcast.14), calls=%async_computation | async-start | bytes 5242880 | tf_op jit(solution)/shard_map/all_to_all | solution.py:399
  17.6 0.0 copy-done.3
  17.6 0.8 copy.14
  18.4 59.7 %all-to-all-done = bf16[32,320,128]{2,1,0:T(8,128)(2,1)S(1)} async-done(((bf16[32,320,128]{2,1,0:T(8,128)(2,1)}), bf16[32,320,128]{2,1,0:T(8,128)(2,1)S(1)}, u32[]{:S(2)}, u32[]{:S(2)}) %all-to-all-start) | async-done | bytes 2621472 | tf_op jit(solution)/shard_map/all_to_all | solution.py:399
  78.0 0.0 copy-start
  78.0 1.5 copy-done
  79.5 34.1 %transfer.1 = (bf16[6144,128]{1,0:T(8,128)(2,1)}, f32[16,3,16,256]{3,2,1,0:T(8,128)}) custom-call(bf16[10240,128]{1,0:T(8,128)(2,1)} %bitcast.12, f32[16,16,256]{2,1,0:T(8,128)} %bitcast.16), custom_call_target="tpu_custom_call" | custom-call | tf_op jit(solution)/shard_map/transfer/pallas_call | solution.py:401
  113.6 0.0 copy-start.2
  113.6 32.0 %all-to-all-start.1 = ((bf16[32,192,128]{2,1,0:T(8,128)(2,1)}), bf16[32,192,128]{2,1,0:T(8,128)(2,1)S(1)}, u32[]{:S(2)}, u32[]{:S(2)}) async-start(bf16[32,192,128]{2,1,0:T(8,128)(2,1)} %bitcast.15), calls=%async_computation.1 | async-start | bytes 3145728 | tf_op jit(solution)/shard_map/all_to_all | solution.py:420
  145.6 0.0 copy-done.2
  145.6 0.1 copy.13
  145.7 1.0 reshape.25
  146.7 38.3 %all-to-all-done.1 = bf16[32,192,128]{2,1,0:T(8,128)(2,1)S(1)} async-done(((bf16[32,192,128]{2,1,0:T(8,128)(2,1)}), bf16[32,192,128]{2,1,0:T(8,128)(2,1)S(1)}, u32[]{:S(2)}, u32[]{:S(2)}) %all-to-all-start.1) | async-done | bytes 1572896 | tf_op jit(solution)/shard_map/all_to_all | solution.py:420
  185.0 0.0 copy-start.1
  185.0 1.1 copy-done.1
  186.2 3.7 %unpack.1 = (f32[3,32768]{1,0:T(4,128)}, f32[9,32768]{1,0:T(8,128)}) custom-call(s32[64]{0:T(128)} %get-tuple-element.11.dest_ref, s32[64]{0:T(128)} %count_ref.3, bf16[6144,128]{1,0:T(8,128)(2,1)} %bitcast.13), custom_call_target="tpu_custom_call" | custom-call | tf_op jit(solution)/shard_map/unpack/pallas_call | solution.py:421
Async XLA Ops:
  5.9 11.6 %copy-start.3 = (f32[16,4096]{1,0:T(8,128)S(1)}, f32[16,4096]{1,0:T(8,128)}, u32[]{:S(2)}) copy-start(f32[16,4096]{1,0:T(8,128)} %param.17) | copy-start | bytes 786436
  5.9 72.1 %all-to-all-start = ((bf16[32,320,128]{2,1,0:T(8,128)(2,1)}), bf16[32,320,128]{2,1,0:T(8,128)(2,1)S(1)}, u32[]{:S(2)}, u32[]{:S(2)}) async-start(bf16[32,320,128]{2,1,0:T(8,128)(2,1)} %bitcast.14), calls=%async_computation | async-start | bytes 5242880 | tf_op jit(solution)/shard_map/all_to_all | solution.py:399
  78.0 1.5 copy-start
  113.6 32.0 %copy-start.2 = (f32[16,3,16,256]{3,2,1,0:T(8,128)S(1)}, f32[16,3,16,256]{3,2,1,0:T(8,128)}, u32[]{:S(2)}) copy-start(f32[16,3,16,256]{3,2,1,0:T(8,128)} %get-tuple-element.10) | copy-start | bytes 2359300
  113.6 71.4 %all-to-all-start.1 = ((bf16[32,192,128]{2,1,0:T(8,128)(2,1)}), bf16[32,192,128]{2,1,0:T(8,128)(2,1)S(1)}, u32[]{:S(2)}, u32[]{:S(2)}) async-start(bf16[32,192,128]{2,1,0:T(8,128)(2,1)} %bitcast.15), calls=%async_computation.1 | async-start | bytes 3145728 | tf_op jit(solution)/shard_map/all_to_all | solution.py:420
  185.0 1.2 copy-start.1

commit v4 on v3

--- a/solution.py
+++ b/solution.py
@@ -14,6 +14,7 @@
 ROWS = 80
 BACK = 48
 CENTER = 7.5
+GROUP = 4
 SMEM = pltpu.SMEM
 VMEM = pltpu.VMEM
 
@@ -239,37 +240,42 @@
     back_ref[pl.ds(first, BACK), :] = jnp.concatenate(eights + merged, axis=0).astype(jnp.bfloat16)
 
 
-def arrivals(data_ref, row_ref, tile_ref, list_ref, sem):
-    slots = row_ref.shape[0]
-
-    def read(slot, carry):
-        first = data_ref[pl.ds(pl.multiple_of(slot * ROWS, 16), 16), :].astype(jnp.float32)
-        row_ref[pl.ds(slot, 1), :] = first[15:16].astype(jnp.int32)
-        return carry
-
-    lax.fori_loop(0, slots, read, 0, unroll=4)
+def arrivals(data_ref, slots, row_ref, tile_ref, sem):
+    lane = lax.broadcasted_iota(jnp.int32, (8, LANES), 1)
+
+    def read(slot, found):
+        rows = data_ref[pl.ds(pl.multiple_of(slot * ROWS, 16), 16), :].astype(jnp.float32)
+        return jnp.where(lane == slot, rows[8:], found)
+
+    found = lax.fori_loop(0, slots, read, jnp.zeros((8, LANES), jnp.float32), unroll=8)
+    row_ref[...] = found.astype(jnp.int32)
     copy = pltpu.make_async_copy(row_ref, tile_ref, sem)
     copy.start()
     copy.wait()
 
-    def collect(slot, count):
-        filled = tile_ref[slot, 0] >= 0
-
-        @pl.when(filled)
+
+def by_group(slots, tile_ref, work):
+    def step(group, carry):
+        first = group * GROUP
+        many = tile_ref[7, first + GROUP // 2] >= 0
+
+        @pl.when(many)
         def _():
-            list_ref[count] = slot
-
-        return count + filled.astype(jnp.int32)
-
-    return lax.fori_loop(0, slots, collect, 0)
-
-
-def main_kernel(
-    data_ref, drag_ref, back_ref, grid_ref, row_ref, tile_ref, list_ref, sums_ref, rows_ref, table, sem, *, parts
-):
+            work(first, GROUP)
+
+        @pl.when(jnp.logical_and(jnp.logical_not(many), tile_ref[7, first] >= 0))
+        def _():
+            work(first, GROUP // 2)
+
+        return carry
+
+    lax.fori_loop(0, slots // GROUP, step, 0)
+
+
+def main_kernel(data_ref, drag_ref, back_ref, grid_ref, row_ref, tile_ref, sums_ref, rows_ref, table, sem, *, parts):
     tiles = drag_ref.shape[0]
-    count = arrivals(data_ref, row_ref, tile_ref, list_ref, sem)
-    pairs = (count + 1) // 2
+    slots = data_ref.shape[0] // ROWS
+    arrivals(data_ref, slots, row_ref, tile_ref, sem)
 
     def clear(tile, carry):
         sums_ref[tile] = jnp.zeros(sums_ref.shape[1:], jnp.float32)
@@ -277,21 +283,14 @@
 
     lax.fori_loop(0, tiles, clear, 0)
 
-    def second_of(pair):
-        return list_ref[jnp.minimum(2 * pair + 1, count - 1)]
-
-    def deposit_pair(pair, carry):
-        first = list_ref[2 * pair]
-        second = second_of(pair)
-        spare = jnp.where(2 * pair + 1 < count, tile_ref[second, 0], tiles)
-        one = deposit_block(data_ref, first, table.at[0], parts)
-        two = deposit_block(data_ref, second, table.at[1], parts)
-        tile = tile_ref[first, 0]
-        sums_ref[tile] = sums_ref[tile] + one
-        sums_ref[spare] = sums_ref[spare] + two
-        return carry
-
-    lax.fori_loop(0, pairs, deposit_pair, 0)
+    def deposit_blocks(first, count):
+        sums = [deposit_block(data_ref, first + k, table.at[k], parts) for k in range(count)]
+        for k in range(count):
+            tile = tile_ref[7, first + k]
+            tile = jnp.where(tile >= 0, tile, tiles)
+            sums_ref[tile] = sums_ref[tile] + sums[k]
+
+    by_group(slots, tile_ref, deposit_blocks)
 
     lane = lax.broadcasted_iota(jnp.int32, (EDGE, PLANE), 1)
     node_y = (lane >> 4).astype(jnp.float32) - CENTER
@@ -316,14 +315,12 @@
 
     lax.fori_loop(0, tiles, update, 0)
 
-    def interpolate_pair(pair, carry):
-        first = list_ref[2 * pair]
-        second = second_of(pair)
-        interpolate_block(data_ref, rows_ref[tile_ref[first, 0]], first, table.at[0], back_ref, parts)
-        interpolate_block(data_ref, rows_ref[tile_ref[second, 0]], second, table.at[1], back_ref, parts)
-        return carry
-
-    lax.fori_loop(0, pairs, interpolate_pair, 0)
+    def interpolate_blocks(first, count):
+        for k in range(count):
+            tile = jnp.maximum(tile_ref[7, first + k], 0)
+            interpolate_block(data_ref, rows_ref[tile], first + k, table.at[k], back_ref, parts)
+
+    by_group(slots, tile_ref, interpolate_blocks)
 
 
 def unpack_kernel(dest_ref, count_ref, back_ref, vel_ref, aff_ref):
@@ -407,16 +404,15 @@
         in_specs=[vmem, vmem],
         out_specs=(vmem, vmem),
         scratch_shapes=[
-            VMEM((slots, LANES), jnp.int32),
-            SMEM((slots, LANES), jnp.int32),
-            SMEM((slots,), jnp.int32),
+            VMEM((8, LANES), jnp.int32),
+            SMEM((8, LANES), jnp.int32),
             VMEM((tiles + 1, 10 * EDGE, PLANE), jnp.float32),
             VMEM((tiles, 5 * span, PLANE), jnp.bfloat16),
-            VMEM((2, TABLE, LANES), jnp.float32),
+            VMEM((GROUP, TABLE, LANES), jnp.float32),
             pltpu.SemaphoreType.DMA,
         ],
         name="transfer",
-    )(arrived, cell_drag.reshape(tiles, EDGE, PLANE))
+    )(pltpu.with_memory_space_constraint(arrived, VMEM), cell_drag.reshape(tiles, EDGE, PLANE))
     returned = lax.all_to_all(back, ("gy", "gz"), split_axis=0, concat_axis=0, tiled=True)
     new_velocity, new_affine = pl.pallas_call(
         unpack_kernel,
@@ -427,7 +423,7 @@
         in_specs=[smem, smem, vmem],
         out_specs=(vmem, vmem),
         name="unpack",
-    )(destination, block_count, returned)
+    )(destination, block_count, pltpu.with_memory_space_constraint(returned, VMEM))
     return (grid.reshape(tiles, 3, EDGE * PLANE), new_velocity, new_affine)
 
 

time: 189 us -> 173 us (0.915)
  starting transfers between devices: 43.6 us -> 33.2 us
  Pallas kernels: 43 us -> 39.9 us
  local copies, waits for them, and re-layouts: 4.55 us -> 1.88 us
    all_to_all x1, starting transfers between devices: 32 us -> 21.5 us  [per_device(): lax.all_to_all(back, ('gy', 'gz'), split_axis=0, concat_axis=0, tiled=True)]
    unnamed x9 -> x5, local copies, waits for them, and re-layouts: 3.47 us -> 0.8 us
    pallas_call x1, Pallas kernels: 34.1 us -> 31.7 us  [per_device(): pl.pallas_call(functools.partial(main_kernel, parts=parts), out_shape=(ja...]
where the time goes in v4:
time: 173 us; the launch traced here: 174 us
  waiting for transfers between devices  98 us (57%)
  Pallas kernels  39.9 us (23%)
  starting transfers between devices  33.2 us (19%)
  local copies, waits for them, and re-layouts  1.88 us (1%)
    all_to_all x1, waiting for transfers between devices, per_device(): lax.all_to_all(outgoing, ('gy', 'gz'), split_axis=0, concat_axis=0, tiled...  59.7 us
    all_to_all x1, waiting for transfers between devices, per_device(): lax.all_to_all(back, ('gy', 'gz'), split_axis=0, concat_axis=0, tiled=True)  38.3 us
    pallas_call x1, Pallas kernels, per_device(): pl.pallas_call(functools.partial(main_kernel, parts=parts), out_shape=(ja...  31.7 us
    all_to_all x1, starting transfers between devices, per_device(): lax.all_to_all(back, ('gy', 'gz'), split_axis=0, concat_axis=0, tiled=True)  21.5 us
    all_to_all x1, starting transfers between devices, per_device(): lax.all_to_all(outgoing, ('gy', 'gz'), split_axis=0, concat_axis=0, tiled...  11.6 us
    pallas_call x1, Pallas kernels, per_device(): pl.pallas_call(functools.partial(pack_kernel, capacity=capacity, group=gr...  5.27 us
  transfers between devices with their start and end apart: 2, of which 2 were waited for; matrix products, arithmetic and copies ran while one was open for 1% of the time, Pallas kernels for 0%

profile of v4, /device:TPU:24, one launch (start us, length us, event | category | flops | bytes accessed | tf_op | source)
XLA Modules:
  0.0 173.6 jit_solution(840609988531651048)
XLA Ops:
  0.6 5.3 %pack.1 = (bf16[10240,128]{1,0:T(8,128)(2,1)}, s32[64]{0:T(128)}) custom-call(s32[64]{0:T(128)} %bitcast.19, s32[64]{0:T(128)} %tile_ref.1, s32[64]{0:T(128)} %count_ref.3, f32[64,4,128]{2,1,0:T(4,128)} %bitcast.18, f32[3,32768]{1,0:T(4,128)} %vel_ref.1, f32[9,32768]{1,0:T(8,128)} %aff_ref.1, s32[3,32768]{1,0:T(4,128)} %cell_ref.1, s32[3,32768]{1,0:T(4,128)} %frac_ref.1), custom_call_target="tpu_custom_call" | custom-call | tf_op jit(solution)/shard_map/pack/pallas_call | solution.py:372
  5.9 0.0 copy-start.1
  5.9 11.6 %all-to-all-start = ((bf16[32,320,128]{2,1,0:T(8,128)(2,1)}), bf16[32,320,128]{2,1,0:T(8,128)(2,1)S(1)}, u32[]{:S(2)}, u32[]{:S(2)}) async-start(bf16[32,320,128]{2,1,0:T(8,128)(2,1)} %bitcast.14), calls=%async_computation | async-start | bytes 5242880 | tf_op jit(solution)/shard_map/all_to_all | solution.py:396
  17.5 0.0 copy-done.1
  17.6 0.8 copy.14
  18.3 59.7 %all-to-all-done = bf16[32,320,128]{2,1,0:T(8,128)(2,1)S(1)} async-done(((bf16[32,320,128]{2,1,0:T(8,128)(2,1)}), bf16[32,320,128]{2,1,0:T(8,128)(2,1)S(1)}, u32[]{:S(2)}, u32[]{:S(2)}) %all-to-all-start) | async-done | bytes 2621472 | tf_op jit(solution)/shard_map/all_to_all | solution.py:396
  78.0 31.7 %transfer.1 = (bf16[6144,128]{1,0:T(8,128)(2,1)}, f32[16,3,16,256]{3,2,1,0:T(8,128)}) custom-call(bf16[10240,128]{1,0:T(8,128)(2,1)S(1)} %bitcast.12, f32[16,16,256]{2,1,0:T(8,128)} %bitcast.16), custom_call_target="tpu_custom_call" | custom-call | tf_op jit(solution)/shard_map/transfer/pallas_call | solution.py:398
  109.7 0.0 copy-start
  109.7 21.5 %all-to-all-start.1 = ((bf16[32,192,128]{2,1,0:T(8,128)(2,1)}), bf16[32,192,128]{2,1,0:T(8,128)(2,1)S(1)}, u32[]{:S(2)}, u32[]{:S(2)}) async-start(bf16[32,192,128]{2,1,0:T(8,128)(2,1)} %bitcast.15), calls=%async_computation.1 | async-start | bytes 3145728 | tf_op jit(solution)/shard_map/all_to_all | solution.py:416
  131.3 0.0 copy-done
  131.3 0.1 copy.13
  131.3 1.0 reshape.25
  132.4 38.3 %all-to-all-done.1 = bf16[32,192,128]{2,1,0:T(8,128)(2,1)S(1)} async-done(((bf16[32,192,128]{2,1,0:T(8,128)(2,1)}), bf16[32,192,128]{2,1,0:T(8,128)(2,1)S(1)}, u32[]{:S(2)}, u32[]{:S(2)}) %all-to-all-start.1) | async-done | bytes 1572896 | tf_op jit(solution)/shard_map/all_to_all | solution.py:416
  170.7 2.9 %unpack.1 = (f32[3,32768]{1,0:T(4,128)}, f32[9,32768]{1,0:T(8,128)}) custom-call(s32[64]{0:T(128)} %get-tuple-element.11.dest_ref, s32[64]{0:T(128)} %count_ref.3, bf16[6144,128]{1,0:T(8,128)(2,1)S(1)} %bitcast.13), custom_call_target="tpu_custom_call" | custom-call | tf_op jit(solution)/shard_map/unpack/pallas_call | solution.py:417
Async XLA Ops:
  5.9 11.6 %copy-start.1 = (f32[16,4096]{1,0:T(8,128)S(1)}, f32[16,4096]{1,0:T(8,128)}, u32[]{:S(2)}) copy-start(f32[16,4096]{1,0:T(8,128)} %param.17) | copy-start | bytes 786436
  5.9 72.1 %all-to-all-start = ((bf16[32,320,128]{2,1,0:T(8,128)(2,1)}), bf16[32,320,128]{2,1,0:T(8,128)(2,1)S(1)}, u32[]{:S(2)}, u32[]{:S(2)}) async-start(bf16[32,320,128]{2,1,0:T(8,128)(2,1)} %bitcast.14), calls=%async_computation | async-start | bytes 5242880 | tf_op jit(solution)/shard_map/all_to_all | solution.py:396
  109.7 21.6 %copy-start = (f32[16,3,16,256]{3,2,1,0:T(8,128)S(1)}, f32[16,3,16,256]{3,2,1,0:T(8,128)}, u32[]{:S(2)}) copy-start(f32[16,3,16,256]{3,2,1,0:T(8,128)} %get-tuple-element.10) | copy-start | bytes 2359300
  109.7 61.0 %all-to-all-start.1 = ((bf16[32,192,128]{2,1,0:T(8,128)(2,1)}), bf16[32,192,128]{2,1,0:T(8,128)(2,1)S(1)}, u32[]{:S(2)}, u32[]{:S(2)}) async-start(bf16[32,192,128]{2,1,0:T(8,128)(2,1)} %bitcast.15), calls=%async_computation.1 | async-start | bytes 3145728 | tf_op jit(solution)/shard_map/all_to_all | solution.py:416

commit v5 on v4

--- a/solution.py
+++ b/solution.py
@@ -14,7 +14,9 @@
 ROWS = 80
 BACK = 48
 CENTER = 7.5
-GROUP = 4
+DEPOSIT_GROUP = 8
+INTERPOLATE_GROUP = 8
+STEPS = 8
 SMEM = pltpu.SMEM
 VMEM = pltpu.VMEM
 
@@ -22,9 +24,10 @@
 def pack_kernel(
     owner_ref, tile_ref, count_ref, mass_ref, vel_ref, aff_ref, cell_ref, frac_ref, out_ref, dest_ref, used_ref, scratch, low_ref, *, capacity, group
 ):
-    blocks = dest_ref.shape[0]
+    blocks = dest_ref.shape[0] // STEPS
     length = vel_ref.shape[1] // blocks
     parts = length // LANES
+    start = pl.program_id(0) * blocks
 
     def clear(owner, carry):
         used_ref[owner] = 0
@@ -33,7 +36,9 @@
             out_ref[pl.ds(first, 16), :] = jnp.full((16, LANES), -1.0, jnp.bfloat16)
         return carry
 
-    lax.fori_loop(0, group, clear, 0)
+    @pl.when(start == 0)
+    def _():
+        lax.fori_loop(0, group, clear, 0)
 
     def place(block):
         owner = owner_ref[block]
@@ -56,8 +61,8 @@
             buffer[3 + 4 * d : 4 + 4 * d, :] = aff_ref[3 * d : 3 * d + 1, where]
         buffer[4:7, :] = vel_ref[:, where]
         buffer[12:15, :] = (code >> 7).astype(jnp.float32)
-        buffer[15:16, :] = jnp.full((1, length), tile_ref[block], jnp.int32).astype(jnp.float32)
-        live = jnp.where(place_in_block < count_ref[block], mass_ref[block], 0.0)
+        buffer[15:16, :] = jnp.full((1, length), tile_ref[start + block], jnp.int32).astype(jnp.float32)
+        live = jnp.where(place_in_block < count_ref[start + block], mass_ref[block], 0.0)
         for part in range(parts):
             lows[4 * part : 4 * part + 3, :] = low[:, part * LANES : (part + 1) * LANES]
             lows[4 * part + 3 : 4 * part + 4, :] = live[part : part + 1]
@@ -68,7 +73,7 @@
         out_ref[pl.ds(pl.multiple_of(first + 16 * parts, 16), 16), :] = lows[...].astype(jnp.bfloat16)
 
     def step(index, carry):
-        slots = [place(index * 2 + k) for k in range(2)]
+        slots = [place(start + index * 2 + k) for k in range(2)]
         for k in range(2):
             move(index * 2 + k, slots[k], scratch.at[k], low_ref.at[k])
         return carry
@@ -89,19 +94,20 @@
     return ref[pl.ds(row, 8, stride=0), :]
 
 
-CELL, FIRST, SECOND, THIRD, MIDDLE, SIDE, NODES = (64 + 16 * k for k in range(7))
-BASE = NODES + 64
+CELL, FIRST, SECOND, THIRD, SIDE = (64 + 16 * k for k in range(5))
+BASE = SIDE + 16
 TABLE = BASE + 32
-
-
-def prepare(data_ref, slot, table, parts, deposit):
+MIDDLE = 192
+KEPT = MIDDLE + 16
+
+
+def prepare(data_ref, slot, table, kept, parts):
     first = pl.multiple_of(slot * ROWS, 16)
     side = data_ref[pl.ds(pl.multiple_of(first + 16 * parts, 16), 16), :].astype(jnp.float32)
     highs = []
     for part in range(parts):
         main = data_ref[pl.ds(pl.multiple_of(first + 16 * part, 16), 16), :].astype(jnp.float32)
-        if deposit:
-            table[16 * part : 16 * part + 16, :] = main
+        table[16 * part : 16 * part + 16, :] = main
         highs.append(main[8:])
     upper = sublanes() < 4
     high = jnp.concatenate(
@@ -115,28 +121,34 @@
     table[FIRST : FIRST + 16, :] = rest * rest
     table[SECOND : SECOND + 16, :] = 1.0 + 2.0 * (inside * rest)
     table[THIRD : THIRD + 16, :] = inside * inside
-    table[MIDDLE : MIDDLE + 16, :] = cell + inside + (0.5 - CENTER)
-    if deposit:
-        table[SIDE : SIDE + 16, :] = side * 0.125
-
-
-def node_weights(table, part, e, nodes):
+    table[SIDE : SIDE + 16, :] = side * 0.125
+    kept[MIDDLE : MIDDLE + 16, :] = cell + inside + (0.5 - CENTER)
+
+
+def node_weights(table, kept, part, e, nodes):
     row = 4 * part + e
     cell = spread(table, CELL + row)
     one, two, three = (spread(table, at + row) for at in (FIRST, SECOND, THIRD))
-    return [
-        jnp.where(cell == node, one, jnp.where(cell == node - 1.0, two, jnp.where(cell == node - 2.0, three, 0.0)))
-        for node in nodes
-    ]
-
-
-def plane_table(table, part, nodes):
-    for half, weight in enumerate(node_weights(table, part, 1, nodes)):
-        table[NODES + 16 * part + 8 * half : NODES + 16 * part + 8 * half + 8, :] = weight
-    upper, lower = node_weights(table, part, 2, nodes)
+    weights = []
+    for half, node in enumerate(nodes):
+        weight = jnp.where(cell == node - 2.0, three, 0.0)
+        weight = jnp.where(cell == node, one, jnp.where(cell == node - 1.0, two, weight))
+        at = 64 * e + 16 * part + 8 * half
+        kept[at : at + 8, :] = weight
+        weights.append(weight)
+    return weights
+
+
+def kept_weights(kept, part, e):
+    at = 64 * e + 16 * part
+    return [kept[at : at + 8, :], kept[at + 8 : at + 16, :]]
+
+
+def plane_table(kept, part, along_z):
+    upper, lower = along_z
     rows = []
     for y in range(EDGE):
-        weight = spread(table, NODES + 16 * part + y)
+        weight = spread(kept, 64 + 16 * part + y)
         rows.append(jnp.concatenate([weight * upper, weight * lower], axis=0).astype(jnp.bfloat16))
     return jnp.concatenate(rows, axis=0)
 
@@ -146,21 +158,22 @@
     return [node, node + 8.0]
 
 
-def deposit_block(data_ref, slot, table, parts):
-    prepare(data_ref, slot, table, parts, True)
+def deposit_block(data_ref, slot, table, kept, parts):
+    prepare(data_ref, slot, table, kept, parts)
     nodes = node_rows()
     leads, planes = [], []
     for part in range(parts):
-        planes.append(plane_table(table, part, nodes))
+        node_weights(table, kept, part, 1, nodes)
+        planes.append(plane_table(kept, part, node_weights(table, kept, part, 2, nodes)))
         row = 4 * part
-        weights = node_weights(table, part, 0, nodes)
-        middle = spread(table, MIDDLE + row)
+        weights = node_weights(table, kept, part, 0, nodes)
+        middle = spread(kept, MIDDLE + row)
         offsets = [(node - CENTER) - middle for node in nodes]
         mass = spread(table, SIDE + row + 3)
         loaded = [mass * weight for weight in weights]
         top = table[16 * part : 16 * part + 8, :]
         bottom = table[16 * part + 8 : 16 * part + 16, :]
-        base = pltpu.roll(top, 4, 0) - top * spread(table, MIDDLE + row + 1) - bottom * spread(table, MIDDLE + row + 2)
+        base = pltpu.roll(top, 4, 0) - top * spread(kept, MIDDLE + row + 1) - bottom * spread(kept, MIDDLE + row + 2)
         table[BASE + 8 * part : BASE + 8 * part + 8, :] = base
         highs, lows = [jnp.concatenate(loaded, axis=0).astype(jnp.bfloat16)], []
 
@@ -198,17 +211,16 @@
     return values[0]
 
 
-def interpolate_block(data_ref, grid_rows, slot, table, back_ref, parts):
-    prepare(data_ref, slot, table, parts, False)
+def interpolate_block(kept, grid_rows, slot, table, back_ref, parts):
     nodes = node_rows()
-    plane = jnp.concatenate([plane_table(table, part, nodes) for part in range(parts)], axis=1)
+    plane = jnp.concatenate([plane_table(kept, part, kept_weights(kept, part, 2)) for part in range(parts)], axis=1)
     moments = jnp.dot(grid_rows, plane, preferred_element_type=jnp.float32)
     span = 3 * EDGE
     row = sublanes()
     eights, fours = [], []
     for part in range(parts):
-        weights = node_weights(table, part, 0, nodes)
-        middle = spread(table, MIDDLE + 4 * part)
+        weights = kept_weights(kept, part, 0)
+        middle = spread(kept, MIDDLE + 4 * part)
         offsets = [(node - CENTER) - middle for node in nodes]
         lanes = slice(part * LANES, (part + 1) * LANES)
         zero, one, two, speed = [], [], [], []
@@ -227,8 +239,8 @@
         four = fold([two[2]] + speed)
         table[BASE + 8 * part : BASE + 8 * part + 8, :] = four
         speeds = [spread(table, BASE + 8 * part + 1 + d) for d in range(3)]
-        center_y = spread(table, MIDDLE + 4 * part + 1)
-        center_z = spread(table, MIDDLE + 4 * part + 2)
+        center_y = spread(kept, MIDDLE + 4 * part + 1)
+        center_z = spread(kept, MIDDLE + 4 * part + 2)
         column = row % 3
         center = jnp.where(column == 1, center_y, jnp.where(column == 2, center_z, 0.0))
         speed = jnp.where(row < 3, speeds[0], jnp.where(row < 6, speeds[1], speeds[2]))
@@ -254,25 +266,34 @@
     copy.wait()
 
 
-def by_group(slots, tile_ref, work):
+def by_group(slots, tile_ref, size, work):
     def step(group, carry):
-        first = group * GROUP
-        many = tile_ref[7, first + GROUP // 2] >= 0
+        first = group * size
+        many = tile_ref[7, first + 2] >= 0
+        for source in range(1, size // 4):
+            many = jnp.logical_and(many, tile_ref[7, first + 4 * source + 2] >= 0)
 
         @pl.when(many)
         def _():
-            work(first, GROUP)
-
-        @pl.when(jnp.logical_and(jnp.logical_not(many), tile_ref[7, first] >= 0))
+            work(first, size)
+
+        @pl.when(jnp.logical_not(many))
         def _():
-            work(first, GROUP // 2)
-
-        return carry
-
-    lax.fori_loop(0, slots // GROUP, step, 0)
-
-
-def main_kernel(data_ref, drag_ref, back_ref, grid_ref, row_ref, tile_ref, sums_ref, rows_ref, table, sem, *, parts):
+            def half(index, carry):
+                @pl.when(tile_ref[7, first + 2 * index] >= 0)
+                def _():
+                    work(first + 2 * index, 2)
+
+                return carry
+
+            lax.fori_loop(0, size // 2, half, 0)
+
+        return carry
+
+    lax.fori_loop(0, slots // size, step, 0)
+
+
+def main_kernel(data_ref, drag_ref, back_ref, grid_ref, row_ref, tile_ref, sums_ref, rows_ref, table, kept_ref, sem, *, parts):
     tiles = drag_ref.shape[0]
     slots = data_ref.shape[0] // ROWS
     arrivals(data_ref, slots, row_ref, tile_ref, sem)
@@ -284,13 +305,13 @@
     lax.fori_loop(0, tiles, clear, 0)
 
     def deposit_blocks(first, count):
-        sums = [deposit_block(data_ref, first + k, table.at[k], parts) for k in range(count)]
+        sums = [deposit_block(data_ref, first + k, table.at[k], kept_ref.at[first + k], parts) for k in range(count)]
         for k in range(count):
             tile = tile_ref[7, first + k]
             tile = jnp.where(tile >= 0, tile, tiles)
             sums_ref[tile] = sums_ref[tile] + sums[k]
 
-    by_group(slots, tile_ref, deposit_blocks)
+    by_group(slots, tile_ref, DEPOSIT_GROUP, deposit_blocks)
 
     lane = lax.broadcasted_iota(jnp.int32, (EDGE, PLANE), 1)
     node_y = (lane >> 4).astype(jnp.float32) - CENTER
@@ -318,22 +339,23 @@
     def interpolate_blocks(first, count):
         for k in range(count):
             tile = jnp.maximum(tile_ref[7, first + k], 0)
-            interpolate_block(data_ref, rows_ref[tile], first + k, table.at[k], back_ref, parts)
-
-    by_group(slots, tile_ref, interpolate_blocks)
+            interpolate_block(kept_ref.at[first + k], rows_ref[tile], first + k, table.at[k], back_ref, parts)
+
+    by_group(slots, tile_ref, INTERPOLATE_GROUP, interpolate_blocks)
 
 
 def unpack_kernel(dest_ref, count_ref, back_ref, vel_ref, aff_ref):
-    blocks = dest_ref.shape[0]
+    blocks = dest_ref.shape[0] // STEPS
     length = vel_ref.shape[1] // blocks
     parts = length // LANES
+    start = pl.program_id(0) * blocks
 
     def one(block):
-        first = pl.multiple_of(dest_ref[block] * BACK, 16)
+        first = pl.multiple_of(dest_ref[start + block] * BACK, 16)
         rows = back_ref[pl.ds(first, BACK), :].astype(jnp.float32)
         for part in range(parts):
             lane = lax.broadcasted_iota(jnp.int32, (8, LANES), 1) + part * LANES
-            present = lane < count_ref[block]
+            present = lane < count_ref[start + block]
             where = pl.ds(pl.multiple_of(block * length + part * LANES, LANES), LANES)
             aff_ref[0:8, where] = jnp.where(present, rows[part * 8 : part * 8 + 8], 0.0)
             rest = jnp.where(present[:4], rows[8 * parts + part * 4 : 8 * parts + part * 4 + 4], 0.0)
@@ -369,13 +391,27 @@
     parts = length // LANES
     smem = pl.BlockSpec(memory_space=SMEM)
     vmem = pl.BlockSpec(memory_space=VMEM)
+
+    def along(rows):
+        return pl.BlockSpec((rows, particles // STEPS), lambda i: (0, i))
+
     outgoing, destination = pl.pallas_call(
         functools.partial(pack_kernel, capacity=capacity, group=group),
         out_shape=(
             jax.ShapeDtypeStruct((slots * ROWS, LANES), jnp.bfloat16),
             jax.ShapeDtypeStruct((blocks,), jnp.int32),
         ),
-        in_specs=[smem, smem, smem, vmem, vmem, vmem, vmem, vmem],
+        grid=(STEPS,),
+        in_specs=[
+            smem,
+            smem,
+            smem,
+            pl.BlockSpec((blocks // STEPS, parts, LANES), lambda i: (i, 0, 0)),
+            along(3),
+            along(9),
+            along(3),
+            along(3),
+        ],
         out_specs=(vmem, smem),
         scratch_shapes=[
             SMEM((group,), jnp.int32),
@@ -408,7 +444,8 @@
             SMEM((8, LANES), jnp.int32),
             VMEM((tiles + 1, 10 * EDGE, PLANE), jnp.float32),
             VMEM((tiles, 5 * span, PLANE), jnp.bfloat16),
-            VMEM((GROUP, TABLE, LANES), jnp.float32),
+            VMEM((DEPOSIT_GROUP, TABLE, LANES), jnp.float32),
+            VMEM((slots, KEPT, LANES), jnp.float32),
             pltpu.SemaphoreType.DMA,
         ],
         name="transfer",
@@ -420,8 +457,9 @@
             jax.ShapeDtypeStruct((3, particles), jnp.float32),
             jax.ShapeDtypeStruct((9, particles), jnp.float32),
         ),
+        grid=(STEPS,),
         in_specs=[smem, smem, vmem],
-        out_specs=(vmem, vmem),
+        out_specs=(along(3), along(9)),
         name="unpack",
     )(destination, block_count, pltpu.with_memory_space_constraint(returned, VMEM))
     return (grid.reshape(tiles, 3, EDGE * PLANE), new_velocity, new_affine)

time: 173 us -> 170 us (0.983); the launches traced: 174 us -> 169 us
  starting transfers between devices: 33.2 us -> 28.6 us
  waiting for transfers between devices: 98 us -> 94.5 us
  Pallas kernels: 39.9 us -> 42.9 us
    all_to_all x1, starting transfers between devices: 21.5 us -> 17 us  [per_device(): lax.all_to_all(back, ('gy', 'gz'), split_axis=0, concat_axis=0, tiled=True)]
    all_to_all x1, waiting for transfers between devices: 38.3 us -> 34.8 us  [per_device(): lax.all_to_all(back, ('gy', 'gz'), split_axis=0, concat_axis=0, tiled=True)]
    pallas_call x1, Pallas kernels: 5.27 us -> 7.28 us  [per_device(): pl.pallas_call(functools.partial(pack_kernel, capacity=capacity, group=gr...]
where the time goes in v5:
time: 170 us; the launch traced here: 169 us
  waiting for transfers between devices  94.5 us (56%)
  Pallas kernels  42.9 us (25%)
  starting transfers between devices  28.6 us (17%)
  local copies, waits for them, and re-layouts  1.88 us (1%)
    all_to_all x1, waiting for transfers between devices, per_device(): lax.all_to_all(outgoing, ('gy', 'gz'), split_axis=0, concat_axis=0, tiled...  59.7 us
    all_to_all x1, waiting for transfers between devices, per_device(): lax.all_to_all(back, ('gy', 'gz'), split_axis=0, concat_axis=0, tiled=True)  34.8 us
    pallas_call x1, Pallas kernels, per_device(): pl.pallas_call(functools.partial(main_kernel, parts=parts), out_shape=(ja...  31.5 us
    all_to_all x1, starting transfers between devices, per_device(): lax.all_to_all(back, ('gy', 'gz'), split_axis=0, concat_axis=0, tiled=True)  17 us
    all_to_all x1, starting transfers between devices, per_device(): lax.all_to_all(outgoing, ('gy', 'gz'), split_axis=0, concat_axis=0, tiled...  11.6 us
    pallas_call x1, Pallas kernels, per_device(): pl.pallas_call(functools.partial(pack_kernel, capacity=capacity, group=gr...  7.28 us
    pallas_call x1, Pallas kernels, per_device(): pl.pallas_call(unpack_kernel, out_shape=(jax.ShapeDtypeStruct((3, particl...  4.12 us
  transfers between devices with their start and end apart: 2, of which 2 were waited for; matrix products, arithmetic and copies ran while one was open for 1% of the time, Pallas kernels for 0%

profile of v5, /device:TPU:24, one launch (start us, length us, event | category | flops | bytes accessed | tf_op | source)
XLA Modules:
  0.0 168.6 jit_solution(10882151724473366327)
XLA Ops:
  0.6 7.3 %pack.1 = (bf16[10240,128]{1,0:T(8,128)(2,1)}, s32[64]{0:T(128)}) custom-call(s32[64]{0:T(128)} %bitcast.19, s32[64]{0:T(128)} %tile_ref.1, s32[64]{0:T(128)} %count_ref.3, f32[64,4,128]{2,1,0:T(4,128)} %bitcast.18, f32[3,32768]{1,0:T(4,128)} %vel_ref.1, f32[9,32768]{1,0:T(8,128)} %aff_ref.1, s32[3,32768]{1,0:T(4,128)} %cell_ref.1, s32[3,32768]{1,0:T(4,128)} %frac_ref.1), custom_call_target="tpu_custom_call" | custom-call | tf_op jit(solution)/shard_map/pack/pallas_call | solution.py:398
  7.9 0.0 copy-start.1
  7.9 11.6 %all-to-all-start = ((bf16[32,320,128]{2,1,0:T(8,128)(2,1)}), bf16[32,320,128]{2,1,0:T(8,128)(2,1)S(1)}, u32[]{:S(2)}, u32[]{:S(2)}) async-start(bf16[32,320,128]{2,1,0:T(8,128)(2,1)} %bitcast.14), calls=%async_computation | async-start | bytes 5242880 | tf_op jit(solution)/shard_map/all_to_all | solution.py:432
  19.6 0.0 copy-done.1
  19.6 0.8 copy.14
  20.4 59.7 %all-to-all-done = bf16[32,320,128]{2,1,0:T(8,128)(2,1)S(1)} async-done(((bf16[32,320,128]{2,1,0:T(8,128)(2,1)}), bf16[32,320,128]{2,1,0:T(8,128)(2,1)S(1)}, u32[]{:S(2)}, u32[]{:S(2)}) %all-to-all-start) | async-done | bytes 2621472 | tf_op jit(solution)/shard_map/all_to_all | solution.py:432
  80.0 31.5 %transfer.1 = (bf16[6144,128]{1,0:T(8,128)(2,1)}, f32[16,3,16,256]{3,2,1,0:T(8,128)}) custom-call(bf16[10240,128]{1,0:T(8,128)(2,1)S(1)} %bitcast.12, f32[16,16,256]{2,1,0:T(8,128)} %bitcast.16), custom_call_target="tpu_custom_call" | custom-call | tf_op jit(solution)/shard_map/transfer/pallas_call | solution.py:434
  111.5 0.0 copy-start
  111.5 17.0 %all-to-all-start.1 = ((bf16[32,192,128]{2,1,0:T(8,128)(2,1)}), bf16[32,192,128]{2,1,0:T(8,128)(2,1)S(1)}, u32[]{:S(2)}, u32[]{:S(2)}) async-start(bf16[32,192,128]{2,1,0:T(8,128)(2,1)} %bitcast.15), calls=%async_computation.1 | async-start | bytes 3145728 | tf_op jit(solution)/shard_map/all_to_all | solution.py:453
  128.5 0.0 copy-done
  128.5 0.1 copy.13
  128.6 1.0 reshape.25
  129.6 34.8 %all-to-all-done.1 = bf16[32,192,128]{2,1,0:T(8,128)(2,1)S(1)} async-done(((bf16[32,192,128]{2,1,0:T(8,128)(2,1)}), bf16[32,192,128]{2,1,0:T(8,128)(2,1)S(1)}, u32[]{:S(2)}, u32[]{:S(2)}) %all-to-all-start.1) | async-done | bytes 1572896 | tf_op jit(solution)/shard_map/all_to_all | solution.py:453
  164.4 4.1 %unpack.1 = (f32[3,32768]{1,0:T(4,128)}, f32[9,32768]{1,0:T(8,128)}) custom-call(s32[64]{0:T(128)} %get-tuple-element.11.dest_ref, s32[64]{0:T(128)} %count_ref.3, bf16[6144,128]{1,0:T(8,128)(2,1)S(1)} %bitcast.13), custom_call_target="tpu_custom_call" | custom-call | tf_op jit(solution)/shard_map/unpack/pallas_call | solution.py:454
Async XLA Ops:
  7.9 11.6 %copy-start.1 = (f32[16,4096]{1,0:T(8,128)S(1)}, f32[16,4096]{1,0:T(8,128)}, u32[]{:S(2)}) copy-start(f32[16,4096]{1,0:T(8,128)} %param.17) | copy-start | bytes 786436
  7.9 72.1 %all-to-all-start = ((bf16[32,320,128]{2,1,0:T(8,128)(2,1)}), bf16[32,320,128]{2,1,0:T(8,128)(2,1)S(1)}, u32[]{:S(2)}, u32[]{:S(2)}) async-start(bf16[32,320,128]{2,1,0:T(8,128)(2,1)} %bitcast.14), calls=%async_computation | async-start | bytes 5242880 | tf_op jit(solution)/shard_map/all_to_all | solution.py:432
  111.5 17.0 %copy-start = (f32[16,3,16,256]{3,2,1,0:T(8,128)S(1)}, f32[16,3,16,256]{3,2,1,0:T(8,128)}, u32[]{:S(2)}) copy-start(f32[16,3,16,256]{3,2,1,0:T(8,128)} %get-tuple-element.10) | copy-start | bytes 2359300
  111.5 52.9 %all-to-all-start.1 = ((bf16[32,192,128]{2,1,0:T(8,128)(2,1)}), bf16[32,192,128]{2,1,0:T(8,128)(2,1)S(1)}, u32[]{:S(2)}, u32[]{:S(2)}) async-start(bf16[32,192,128]{2,1,0:T(8,128)(2,1)} %bitcast.15), calls=%async_computation.1 | async-start | bytes 3145728 | tf_op jit(solution)/shard_map/all_to_all | solution.py:453

commit v6 on v5

--- a/solution.py
+++ b/solution.py
@@ -14,9 +14,8 @@
 ROWS = 80
 BACK = 48
 CENTER = 7.5
-DEPOSIT_GROUP = 8
+DEPOSIT_GROUP = 16
 INTERPOLATE_GROUP = 8
-STEPS = 8
 SMEM = pltpu.SMEM
 VMEM = pltpu.VMEM
 
@@ -24,10 +23,9 @@
 def pack_kernel(
     owner_ref, tile_ref, count_ref, mass_ref, vel_ref, aff_ref, cell_ref, frac_ref, out_ref, dest_ref, used_ref, scratch, low_ref, *, capacity, group
 ):
-    blocks = dest_ref.shape[0] // STEPS
+    blocks = dest_ref.shape[0]
     length = vel_ref.shape[1] // blocks
     parts = length // LANES
-    start = pl.program_id(0) * blocks
 
     def clear(owner, carry):
         used_ref[owner] = 0
@@ -36,9 +34,7 @@
             out_ref[pl.ds(first, 16), :] = jnp.full((16, LANES), -1.0, jnp.bfloat16)
         return carry
 
-    @pl.when(start == 0)
-    def _():
-        lax.fori_loop(0, group, clear, 0)
+    lax.fori_loop(0, group, clear, 0)
 
     def place(block):
         owner = owner_ref[block]
@@ -61,8 +57,8 @@
             buffer[3 + 4 * d : 4 + 4 * d, :] = aff_ref[3 * d : 3 * d + 1, where]
         buffer[4:7, :] = vel_ref[:, where]
         buffer[12:15, :] = (code >> 7).astype(jnp.float32)
-        buffer[15:16, :] = jnp.full((1, length), tile_ref[start + block], jnp.int32).astype(jnp.float32)
-        live = jnp.where(place_in_block < count_ref[start + block], mass_ref[block], 0.0)
+        buffer[15:16, :] = jnp.full((1, length), tile_ref[block], jnp.int32).astype(jnp.float32)
+        live = jnp.where(place_in_block < count_ref[block], mass_ref[block], 0.0)
         for part in range(parts):
             lows[4 * part : 4 * part + 3, :] = low[:, part * LANES : (part + 1) * LANES]
             lows[4 * part + 3 : 4 * part + 4, :] = live[part : part + 1]
@@ -73,12 +69,12 @@
         out_ref[pl.ds(pl.multiple_of(first + 16 * parts, 16), 16), :] = lows[...].astype(jnp.bfloat16)
 
     def step(index, carry):
-        slots = [place(start + index * 2 + k) for k in range(2)]
-        for k in range(2):
-            move(index * 2 + k, slots[k], scratch.at[k], low_ref.at[k])
-        return carry
-
-    lax.fori_loop(0, blocks // 2, step, 0)
+        slots = [place(index * 4 + k) for k in range(4)]
+        for k in range(4):
+            move(index * 4 + k, slots[k], scratch.at[k], low_ref.at[k])
+        return carry
+
+    lax.fori_loop(0, blocks // 4, step, 0)
 
 
 def split(value):
@@ -266,12 +262,11 @@
     copy.wait()
 
 
-def by_group(slots, tile_ref, size, work):
+def by_group(slots, tile_ref, size, least, work):
     def step(group, carry):
         first = group * size
-        many = tile_ref[7, first + 2] >= 0
-        for source in range(1, size // 4):
-            many = jnp.logical_and(many, tile_ref[7, first + 4 * source + 2] >= 0)
+        filled = [tile_ref[7, first + 2 * index] >= 0 for index in range(size // 2)]
+        many = sum(one.astype(jnp.int32) for one in filled) >= least
 
         @pl.when(many)
         def _():
@@ -279,14 +274,14 @@
 
         @pl.when(jnp.logical_not(many))
         def _():
-            def half(index, carry):
+            def pair(index, carry):
                 @pl.when(tile_ref[7, first + 2 * index] >= 0)
                 def _():
                     work(first + 2 * index, 2)
 
                 return carry
 
-            lax.fori_loop(0, size // 2, half, 0)
+            lax.fori_loop(0, size // 2, pair, 0)
 
         return carry
 
@@ -311,7 +306,7 @@
             tile = jnp.where(tile >= 0, tile, tiles)
             sums_ref[tile] = sums_ref[tile] + sums[k]
 
-    by_group(slots, tile_ref, DEPOSIT_GROUP, deposit_blocks)
+    by_group(slots, tile_ref, DEPOSIT_GROUP, 6, deposit_blocks)
 
     lane = lax.broadcasted_iota(jnp.int32, (EDGE, PLANE), 1)
     node_y = (lane >> 4).astype(jnp.float32) - CENTER
@@ -341,21 +336,20 @@
             tile = jnp.maximum(tile_ref[7, first + k], 0)
             interpolate_block(kept_ref.at[first + k], rows_ref[tile], first + k, table.at[k], back_ref, parts)
 
-    by_group(slots, tile_ref, INTERPOLATE_GROUP, interpolate_blocks)
+    by_group(slots, tile_ref, INTERPOLATE_GROUP, 4, interpolate_blocks)
 
 
 def unpack_kernel(dest_ref, count_ref, back_ref, vel_ref, aff_ref):
-    blocks = dest_ref.shape[0] // STEPS
+    blocks = dest_ref.shape[0]
     length = vel_ref.shape[1] // blocks
     parts = length // LANES
-    start = pl.program_id(0) * blocks
 
     def one(block):
-        first = pl.multiple_of(dest_ref[start + block] * BACK, 16)
+        first = pl.multiple_of(dest_ref[block] * BACK, 16)
         rows = back_ref[pl.ds(first, BACK), :].astype(jnp.float32)
         for part in range(parts):
             lane = lax.broadcasted_iota(jnp.int32, (8, LANES), 1) + part * LANES
-            present = lane < count_ref[start + block]
+            present = lane < count_ref[block]
             where = pl.ds(pl.multiple_of(block * length + part * LANES, LANES), LANES)
             aff_ref[0:8, where] = jnp.where(present, rows[part * 8 : part * 8 + 8], 0.0)
             rest = jnp.where(present[:4], rows[8 * parts + part * 4 : 8 * parts + part * 4 + 4], 0.0)
@@ -363,11 +357,11 @@
             vel_ref[:, where] = rest[1:4]
 
     def step(index, carry):
-        for k in range(2):
-            one(index * 2 + k)
-        return carry
-
-    lax.fori_loop(0, blocks // 2, step, 0)
+        for k in range(4):
+            one(index * 4 + k)
+        return carry
+
+    lax.fori_loop(0, blocks // 4, step, 0)
 
 
 def per_device(
@@ -391,32 +385,18 @@
     parts = length // LANES
     smem = pl.BlockSpec(memory_space=SMEM)
     vmem = pl.BlockSpec(memory_space=VMEM)
-
-    def along(rows):
-        return pl.BlockSpec((rows, particles // STEPS), lambda i: (0, i))
-
     outgoing, destination = pl.pallas_call(
         functools.partial(pack_kernel, capacity=capacity, group=group),
         out_shape=(
             jax.ShapeDtypeStruct((slots * ROWS, LANES), jnp.bfloat16),
             jax.ShapeDtypeStruct((blocks,), jnp.int32),
         ),
-        grid=(STEPS,),
-        in_specs=[
-            smem,
-            smem,
-            smem,
-            pl.BlockSpec((blocks // STEPS, parts, LANES), lambda i: (i, 0, 0)),
-            along(3),
-            along(9),
-            along(3),
-            along(3),
-        ],
+        in_specs=[smem, smem, smem, vmem, vmem, vmem, vmem, vmem],
         out_specs=(vmem, smem),
         scratch_shapes=[
             SMEM((group,), jnp.int32),
-            VMEM((2, 16, length), jnp.float32),
-            VMEM((2, 16, LANES), jnp.float32),
+            VMEM((4, 16, length), jnp.float32),
+            VMEM((4, 16, LANES), jnp.float32),
         ],
         name="pack",
     )(
@@ -457,9 +437,8 @@
             jax.ShapeDtypeStruct((3, particles), jnp.float32),
             jax.ShapeDtypeStruct((9, particles), jnp.float32),
         ),
-        grid=(STEPS,),
         in_specs=[smem, smem, vmem],
-        out_specs=(along(3), along(9)),
+        out_specs=(vmem, vmem),
         name="unpack",
     )(destination, block_count, pltpu.with_memory_space_constraint(returned, VMEM))
     return (grid.reshape(tiles, 3, EDGE * PLANE), new_velocity, new_affine)

time: 170 us -> 166 us (0.976)
  starting transfers between devices: 28.6 us -> 25.2 us
  waiting for transfers between devices: 94.5 us -> 96.9 us
    all_to_all x1, starting transfers between devices: 17 us -> 13.6 us  [per_device(): lax.all_to_all(back, ('gy', 'gz'), split_axis=0, concat_axis=0, tiled=True)]
    all_to_all x1, waiting for transfers between devices: 34.8 us -> 37.2 us  [per_device(): lax.all_to_all(back, ('gy', 'gz'), split_axis=0, concat_axis=0, tiled=True)]
    pallas_call x1, Pallas kernels: 7.28 us -> 5.19 us  [per_device(): pl.pallas_call(functools.partial(pack_kernel, capacity=capacity, group=gr...]
where the time goes in v6:
time: 166 us
  waiting for transfers between devices  96.9 us (58%)
  Pallas kernels  41.3 us (25%)
  starting transfers between devices  25.2 us (15%)
  local copies, waits for them, and re-layouts  1.88 us (1%)
    all_to_all x1, waiting for transfers between devices, per_device(): lax.all_to_all(outgoing, ('gy', 'gz'), split_axis=0, concat_axis=0, tiled...  59.7 us
    all_to_all x1, waiting for transfers between devices, per_device(): lax.all_to_all(back, ('gy', 'gz'), split_axis=0, concat_axis=0, tiled=True)  37.2 us
    pallas_call x1, Pallas kernels, per_device(): pl.pallas_call(functools.partial(main_kernel, parts=parts), out_shape=(ja...  33.1 us
    all_to_all x1, starting transfers between devices, per_device(): lax.all_to_all(back, ('gy', 'gz'), split_axis=0, concat_axis=0, tiled=True)  13.6 us
    all_to_all x1, starting transfers between devices, per_device(): lax.all_to_all(outgoing, ('gy', 'gz'), split_axis=0, concat_axis=0, tiled...  11.6 us
    pallas_call x1, Pallas kernels, per_device(): pl.pallas_call(functools.partial(pack_kernel, capacity=capacity, group=gr...  5.19 us
  transfers between devices with their start and end apart: 2, of which 2 were waited for; matrix products, arithmetic and copies ran while one was open for 1% of the time, Pallas kernels for 0%

profile of v6, /device:TPU:24, one launch (start us, length us, event | category | flops | bytes accessed | tf_op | source)
XLA Modules:
  0.0 166.0 jit_solution(3578380425378840287)
XLA Ops:
  0.6 5.2 %pack.1 = (bf16[10240,128]{1,0:T(8,128)(2,1)}, s32[64]{0:T(128)}) custom-call(s32[64]{0:T(128)} %bitcast.19, s32[64]{0:T(128)} %tile_ref.1, s32[64]{0:T(128)} %count_ref.3, f32[64,4,128]{2,1,0:T(4,128)} %bitcast.18, f32[3,32768]{1,0:T(4,128)} %vel_ref.1, f32[9,32768]{1,0:T(8,128)} %aff_ref.1, s32[3,32768]{1,0:T(4,128)} %cell_ref.1, s32[3,32768]{1,0:T(4,128)} %frac_ref.1), custom_call_target="tpu_custom_call" | custom-call | tf_op jit(solution)/shard_map/pack/pallas_call | solution.py:388
  5.8 0.0 copy-start.1
  5.8 11.6 %all-to-all-start = ((bf16[32,320,128]{2,1,0:T(8,128)(2,1)}), bf16[32,320,128]{2,1,0:T(8,128)(2,1)S(1)}, u32[]{:S(2)}, u32[]{:S(2)}) async-start(bf16[32,320,128]{2,1,0:T(8,128)(2,1)} %bitcast.14), calls=%async_computation | async-start | bytes 5242880 | tf_op jit(solution)/shard_map/all_to_all | solution.py:412
  17.5 0.0 copy-done.1
  17.5 0.8 copy.14
  18.3 59.7 %all-to-all-done = bf16[32,320,128]{2,1,0:T(8,128)(2,1)S(1)} async-done(((bf16[32,320,128]{2,1,0:T(8,128)(2,1)}), bf16[32,320,128]{2,1,0:T(8,128)(2,1)S(1)}, u32[]{:S(2)}, u32[]{:S(2)}) %all-to-all-start) | async-done | bytes 2621472 | tf_op jit(solution)/shard_map/all_to_all | solution.py:412
  77.9 33.1 %transfer.1 = (bf16[6144,128]{1,0:T(8,128)(2,1)}, f32[16,3,16,256]{3,2,1,0:T(8,128)}) custom-call(bf16[10240,128]{1,0:T(8,128)(2,1)S(1)} %bitcast.12, f32[16,16,256]{2,1,0:T(8,128)} %bitcast.16), custom_call_target="tpu_custom_call" | custom-call | tf_op jit(solution)/shard_map/transfer/pallas_call | solution.py:414
  111.1 0.0 copy-start
  111.1 13.6 %all-to-all-start.1 = ((bf16[32,192,128]{2,1,0:T(8,128)(2,1)}), bf16[32,192,128]{2,1,0:T(8,128)(2,1)S(1)}, u32[]{:S(2)}, u32[]{:S(2)}) async-start(bf16[32,192,128]{2,1,0:T(8,128)(2,1)} %bitcast.15), calls=%async_computation.1 | async-start | bytes 3145728 | tf_op jit(solution)/shard_map/all_to_all | solution.py:433
  124.7 0.0 copy-done
  124.7 0.1 copy.13
  124.8 1.0 reshape.25
  125.8 37.2 %all-to-all-done.1 = bf16[32,192,128]{2,1,0:T(8,128)(2,1)S(1)} async-done(((bf16[32,192,128]{2,1,0:T(8,128)(2,1)}), bf16[32,192,128]{2,1,0:T(8,128)(2,1)S(1)}, u32[]{:S(2)}, u32[]{:S(2)}) %all-to-all-start.1) | async-done | bytes 1572896 | tf_op jit(solution)/shard_map/all_to_all | solution.py:433
  163.0 3.0 %unpack.1 = (f32[3,32768]{1,0:T(4,128)}, f32[9,32768]{1,0:T(8,128)}) custom-call(s32[64]{0:T(128)} %get-tuple-element.11.dest_ref, s32[64]{0:T(128)} %count_ref.3, bf16[6144,128]{1,0:T(8,128)(2,1)S(1)} %bitcast.13), custom_call_target="tpu_custom_call" | custom-call | tf_op jit(solution)/shard_map/unpack/pallas_call | solution.py:434
Async XLA Ops:
  5.8 11.6 %copy-start.1 = (f32[16,4096]{1,0:T(8,128)S(1)}, f32[16,4096]{1,0:T(8,128)}, u32[]{:S(2)}) copy-start(f32[16,4096]{1,0:T(8,128)} %param.17) | copy-start | bytes 786436
  5.8 72.1 %all-to-all-start = ((bf16[32,320,128]{2,1,0:T(8,128)(2,1)}), bf16[32,320,128]{2,1,0:T(8,128)(2,1)S(1)}, u32[]{:S(2)}, u32[]{:S(2)}) async-start(bf16[32,320,128]{2,1,0:T(8,128)(2,1)} %bitcast.14), calls=%async_computation | async-start | bytes 5242880 | tf_op jit(solution)/shard_map/all_to_all | solution.py:412
  111.1 13.6 %copy-start = (f32[16,3,16,256]{3,2,1,0:T(8,128)S(1)}, f32[16,3,16,256]{3,2,1,0:T(8,128)}, u32[]{:S(2)}) copy-start(f32[16,3,16,256]{3,2,1,0:T(8,128)} %get-tuple-element.10) | copy-start | bytes 2359300
  111.1 51.9 %all-to-all-start.1 = ((bf16[32,192,128]{2,1,0:T(8,128)(2,1)}), bf16[32,192,128]{2,1,0:T(8,128)(2,1)S(1)}, u32[]{:S(2)}, u32[]{:S(2)}) async-start(bf16[32,192,128]{2,1,0:T(8,128)(2,1)} %bitcast.15), calls=%async_computation.1 | async-start | bytes 3145728 | tf_op jit(solution)/shard_map/all_to_all | solution.py:433
